TPU v7x, 32 devices: a whole 2x2x4 slice. The times are simulated.
32 devices in a mesh: node: 4 (over x, core), space: 8 (over z, y).
Axes of the slice: x: 2, y: 2, z: 4, core: 2. Of those that a mesh axis runs over, the one named last changes fastest.
Arguments:
- initial: float32 [32, 256, 256], P('space'), may hold values from -1 to 1
- kappa: float32 [32, 256, 256], P('space'), may hold values from 0.3 to 3
Outputs:
- sections: float32 [4, 32, 256, 256], P('node', 'space')
All inputs are finite; a program needn't handle non-finite values.
Results may differ from a plain program's by a relative error of at most 0.0002.
Values sent between devices are 32-bit elements; how exact they have to be, the bound alone decides.
A program may use at most 192 MiB of HBM per device.

v0:
```python
import jax
import jax.numpy as jnp
from jax import lax
from jax.sharding import PartitionSpec as P

SWEEPS = 2
VCYCLES = 2
SMOOTH = 2
LEVELS = 3
COARSE = 8


DIFFUSE = 2.0
REACT = 0.5
OMEGA = 0.8


def extended(cells, sides, width):
    for axis, dim in sides:
        count = lax.axis_size(axis)
        head = lax.slice_in_dim(cells, 0, width, axis=dim)
        tail = lax.slice_in_dim(cells, cells.shape[dim] - width, cells.shape[dim], axis=dim)
        cells = jnp.concatenate(
            [
                lax.ppermute(tail, axis, [(i, (i + 1) % count) for i in range(count)]),
                cells,
                lax.ppermute(head, axis, [((i + 1) % count, i) for i in range(count)]),
            ],
            axis=dim,
        )
    return cells


def radau_gap(count, where):
    previous = 1.0
    current = where
    for degree in range(1, count):
        following = ((2 * degree + 1) * where * current - degree * previous) / (degree + 1)
        previous = current
        current = following
    return current - previous


def radau_table(count):
    zeros_found = []
    grid_count = 4096
    lower = -1.0
    value_low = radau_gap(count, lower)
    for place in range(1, grid_count):
        upper = -1.0 + 2.0 * place / grid_count
        value_up = radau_gap(count, upper)
        if value_low * value_up < 0.0:
            left_end = lower
            right_end = upper
            left_value = value_low
            for halving in range(100):
                middle = 0.5 * (left_end + right_end)
                middle_value = radau_gap(count, middle)
                if left_value * middle_value <= 0.0:
                    right_end = middle
                else:
                    left_end = middle
                    left_value = middle_value
            zeros_found.append(0.5 * (left_end + right_end))
        lower = upper
        value_low = value_up
    zeros_found.append(1.0)
    abscissa = [(value + 1.0) / 2.0 for value in zeros_found]
    table_rows = []
    for outer in range(count):
        table_rows.append([0.0] * count)
    for column in range(count):
        factor = [1.0]
        scale = 1.0
        for other in range(count):
            if other != column:
                widened = [0.0] * (len(factor) + 1)
                for power in range(len(factor)):
                    widened[power + 1] = widened[power + 1] + factor[power]
                    widened[power] = widened[power] - abscissa[other] * factor[power]
                factor = widened
                scale = scale * (abscissa[column] - abscissa[other])
        for outer in range(count):
            upto = abscissa[outer]
            accum = 0.0
            for power in range(len(factor)):
                accum = accum + factor[power] * upto ** (power + 1) / (power + 1)
            table_rows[outer][column] = accum / scale
    return (abscissa, table_rows)


def inner_stencil(padded):
    middle = padded[:, 1:-1]
    total = padded[:, 2:] + padded[:, :-2]
    total = total + jnp.roll(middle, 1, 2) + jnp.roll(middle, -1, 2)
    total = total + jnp.roll(middle, 1, 3) + jnp.roll(middle, -1, 3)
    return total - 6.0 * middle


def stencil(field):
    padded = extended(field, (("space", 1),), 1)
    return inner_stencil(padded)


def smooth(field, source, shift):
    applied = field - shift * stencil(field)
    return field + OMEGA * (source - applied) / (1.0 + 6.0 * shift)


def restrict(field):
    a, b, c, d = field.shape
    return field.reshape(a, b // 2, 2, c // 2, 2, d // 2, 2).mean(axis=(2, 4, 6))


def prolong(field):
    return jnp.repeat(jnp.repeat(jnp.repeat(field, 2, 1), 2, 2), 2, 3)


def coarsest(source, shift):
    field = jnp.zeros_like(source)
    for sweep in range(COARSE):
        field = smooth(field, source, shift)
    return field


def vcycle(level, field, source, shift):
    if level == LEVELS - 1:
        return coarsest(source, shift)
    if field is None:
        field = jnp.zeros_like(source)
    for sweep in range(SMOOTH):
        field = smooth(field, source, shift)
    remain = source - (field - shift * stencil(field))
    coarse_part = vcycle(level + 1, None, restrict(remain), shift / 4.0)
    field = field + prolong(coarse_part)
    for sweep in range(SMOOTH):
        field = smooth(field, source, shift)
    return field


def per_device(initial, kappa):
    count = lax.axis_size("node")
    position = lax.axis_index("node")
    abscissa, table_rows = radau_table(count)
    table = jnp.asarray(table_rows, jnp.float32)
    shift = jnp.asarray([DIFFUSE * value for value in abscissa], jnp.float32)[position]
    section = initial[None]
    strength = kappa[None]
    for sweep in range(SWEEPS):
        lap = stencil(section)
        force = DIFFUSE * lap + REACT * strength * (section - section * section * section)
        weight_row = table[position]
        piece = lax.all_gather(force, "node", axis=0, tiled=True)
        weights = lax.slice_in_dim(weight_row, 0, piece.shape[0], axis=0)
        integral = jnp.zeros_like(force) + jnp.sum(
            weights[:, None, None, None] * piece, axis=0, keepdims=True
        )
        right = initial[None] + integral - shift * lap
        for cycle in range(VCYCLES):
            section = vcycle(0, section, right, shift)
    return section


def solution(mesh):
    in_specs = (P("space", None, None), P("space", None, None))
    out_specs = P("node", "space", None, None)
    return jax.shard_map(
        per_device, mesh=mesh, in_specs=in_specs, out_specs=out_specs, check_vma=False
    )
```

profile of v0, /device:TPU:0, one launch (start us, length us, event | category | flops | bytes accessed | tf_op | source)
XLA Modules:
  0.0 1127.6 jit_solution(7866949773169772399)
XLA Ops:
  16.2 5.8 collective-permute-done.1
  36.1 24.6 %all-gather.3.cloned.1.call-done = f32[4,4,256,256]{3,2,1,0:T(8,128)} async-done(((f32[1,4,256,256]{3,2,1,0:T(8,128)}), f32[4,4,256,256]{3,2,1,0:T(8,128)}) %all-gather.3.cloned.1.call-update) | async-done | bytes 4194320 | tf_op jit(solution)/shard_map/all_gather | solution.py:153
  69.9 8.1 collective-permute-done.3
  87.3 6.1 collective-permute-done.5
  98.3 68.4 %reshape.213 = f32[2,2,128,2,128,2]{5,4,3,2,1,0:T(8,128)} reshape(f32[1,4,256,256]{3,2,1,0:T(8,128)S(1)} %fusion.202) | data formatting | bytes 2097152 | tf_op jit(solution)/shard_map/reshape | solution.py:112
  166.7 20.8 %reduce_sum.101 = f32[2,128,128]{2,1,0:T(8,128)S(1)} reduce(f32[2,2,128,2,128,2]{5,4,3,2,1,0:T(8,128)} %reshape.213, f32[]{:T(128)} %constant.56.clone.1), dimensions={1,3,5}, to_apply=%region_1.2 | reduce | flops 229376 | bytes 1179652 | tf_op jit(solution)/shard_map/reduce_sum | solution.py:112
  202.5 5.6 reduce_sum.121
  303.3 5.2 collective-permute-done.35
  334.0 5.8 collective-permute-done.39
  357.9 68.4 %reshape.214 = f32[2,2,128,2,128,2]{5,4,3,2,1,0:T(8,128)} reshape(f32[1,4,256,256]{3,2,1,0:T(8,128)S(1)} %fusion.145) | data formatting | bytes 2097152 | tf_op jit(solution)/shard_map/reshape | solution.py:112
  426.3 20.8 %reduce_sum.123 = f32[2,128,128]{2,1,0:T(8,128)S(1)} reduce(f32[2,2,128,2,128,2]{5,4,3,2,1,0:T(8,128)} %reshape.214, f32[]{:T(128)} %constant.56.clone.1), dimensions={1,3,5}, to_apply=%region_4.5 | reduce | flops 229376 | bytes 1179652 | tf_op jit(solution)/shard_map/reduce_sum | solution.py:112
  462.0 5.6 reduce_sum.125
  579.8 34.9 %all-gather.5.cloned.1.call-done = f32[4,4,256,256]{3,2,1,0:T(8,128)} async-done(((f32[1,4,256,256]{3,2,1,0:T(8,128)}), f32[4,4,256,256]{3,2,1,0:T(8,128)}) %all-gather.5.cloned.1.call-update) | async-done | bytes 4194320 | tf_op jit(solution)/shard_map/all_gather | solution.py:153
  624.1 8.1 collective-permute-done.71
  641.5 6.1 collective-permute-done.73
  652.5 68.4 %reshape.215 = f32[2,2,128,2,128,2]{5,4,3,2,1,0:T(8,128)} reshape(f32[1,4,256,256]{3,2,1,0:T(8,128)S(1)} %fusion.94) | data formatting | bytes 2097152 | tf_op jit(solution)/shard_map/reshape | solution.py:112
  720.9 20.8 %reduce_sum.128 = f32[2,128,128]{2,1,0:T(8,128)S(1)} reduce(f32[2,2,128,2,128,2]{5,4,3,2,1,0:T(8,128)} %reshape.215, f32[]{:T(128)} %constant.56.clone.1), dimensions={1,3,5}, to_apply=%region_8.9 | reduce | flops 229376 | bytes 1179652 | tf_op jit(solution)/shard_map/reduce_sum | solution.py:112
  756.5 5.6 reduce_sum.130
  855.6 5.8 collective-permute-done.99
  871.0 5.4 collective-permute-done.101
  887.9 6.3 collective-permute-done.103
  911.8 68.4 %reshape.216 = f32[2,2,128,2,128,2]{5,4,3,2,1,0:T(8,128)} reshape(f32[1,4,256,256]{3,2,1,0:T(8,128)S(1)} %fusion.37) | data formatting | bytes 2097152 | tf_op jit(solution)/shard_map/reshape | solution.py:112
  980.2 20.8 %reduce_sum.132 = f32[2,128,128]{2,1,0:T(8,128)S(1)} reduce(f32[2,2,128,2,128,2]{5,4,3,2,1,0:T(8,128)} %reshape.216, f32[]{:T(128)} %constant.56.clone.1), dimensions={1,3,5}, to_apply=%region_11.12 | reduce | flops 229376 | bytes 1179652 | tf_op jit(solution)/shard_map/reduce_sum | solution.py:112
  1015.9 5.6 reduce_sum.134
  (698 shorter events, 607.2 us)
Async XLA Ops:
  6.5 54.1 %all-gather.3.cloned.1.call-start = ((), (), s32[]{:S(2)}) async-start(), calls=%async_computation | async-start | bytes 5242880 | tf_op jit(solution)/shard_map/all_gather | solution.py:153
  7.7 14.2 %collective-permute-start.1 = (f32[1,1,256,256]{3,2,1,0:T(8,128)S(1)}, f32[1,1,256,256]{3,2,1,0:T(8,128)S(1)}, u32[]{:S(2)}, u32[]{:S(2)}) collective-permute-start(f32[1,1,256,256]{3,2,1,0:T(8,128)S(1)} %get-tuple-element.208), channel_id=1, source_target_pairs={{0,1},{1,2},{2,3},{3,4},{4,5},{5,6},{6,7},{7,0},{8,9},{9,10},{10,1... | collective-permute-start | bytes 786440 | tf_op jit(solution)/shard_map/ppermute | solution.py:25
  10.7 13.4 %collective-permute-start = (f32[1,1,256,256]{3,2,1,0:T(8,128)S(1)}, f32[1,1,256,256]{3,2,1,0:T(8,128)S(1)}, u32[]{:S(2)}, u32[]{:S(2)}) collective-permute-start(f32[1,1,256,256]{3,2,1,0:T(8,128)S(1)} %get-tuple-element.207), channel_id=1, source_target_pairs={{1,0},{2,1},{3,2},{4,3},{5,4},{6,5},{7,6},{0,7},{9,8},{10,9},{11,1... | collective-permute-start | bytes 786440 | tf_op jit(solution)/shard_map/ppermute | solution.py:27
  26.0 588.7 %all-gather.5.cloned.1.call-start = ((), (), s32[]{:S(2)}) async-start(), calls=%async_computation.1 | async-start | bytes 5242880 | tf_op jit(solution)/shard_map/all_gather | solution.py:153
  26.1 161.4 %collective-permute-start.7 = (f32[1,1,128,128]{3,2,1,0:T(8,128)S(1)}, f32[1,1,128,128]{3,2,1,0:T(8,128)S(1)}, u32[]{:S(2)}, u32[]{:S(2)}) collective-permute-start(f32[1,1,128,128]{3,2,1,0:T(8,128)S(1)} %broadcast.254), channel_id=1, source_target_pairs={{0,1},{1,2},{2,3},{3,4},{4,5},{5,6},{6,7},{7,0},{8,9},{9,10},{10,1... | collective-permute-start | bytes 196616 | tf_op jit(solution)/shard_map/ppermute | solution.py:25
  26.5 161.0 %collective-permute-start.6 = (f32[1,1,128,128]{3,2,1,0:T(8,128)S(1)}, f32[1,1,128,128]{3,2,1,0:T(8,128)S(1)}, u32[]{:S(2)}, u32[]{:S(2)}) collective-permute-start(f32[1,1,128,128]{3,2,1,0:T(8,128)S(1)} %broadcast.254), channel_id=1, source_target_pairs={{1,0},{2,1},{3,2},{4,3},{5,4},{6,5},{7,6},{0,7},{9,8},{10,9},{11,1... | collective-permute-start | bytes 196616 | tf_op jit(solution)/shard_map/ppermute | solution.py:27
  30.9 180.0 %collective-permute-start.12 = (f32[1,1,64,64]{3,2,1,0:T(8,128)S(1)}, f32[1,1,64,64]{3,2,1,0:T(8,128)S(1)}, u32[]{:S(2)}, u32[]{:S(2)}) collective-permute-start(f32[1,1,64,64]{3,2,1,0:T(8,128)S(1)} %broadcast.258), channel_id=1, source_target_pairs={{1,0},{2,1},{3,2},{4,3},{5,4},{6,5},{7,6},{0,7},{9,8},{10,9},{11,1... | collective-permute-start | bytes 49160 | tf_op jit(solution)/shard_map/ppermute | solution.py:27
  65.0 13.1 %collective-permute-start.3 = (f32[1,1,256,256]{3,2,1,0:T(8,128)S(1)}, f32[1,1,256,256]{3,2,1,0:T(8,128)S(1)}, u32[]{:S(2)}, u32[]{:S(2)}) collective-permute-start(f32[1,1,256,256]{3,2,1,0:T(8,128)S(1)} %get-tuple-element.206), channel_id=1, source_target_pairs={{0,1},{1,2},{2,3},{3,4},{4,5},{5,6},{6,7},{7,0},{8,9},{9,10},{10,1... | collective-permute-start | bytes 786440 | tf_op jit(solution)/shard_map/ppermute | solution.py:25
  66.5 13.8 %collective-permute-start.2 = (f32[1,1,256,256]{3,2,1,0:T(8,128)S(1)}, f32[1,1,256,256]{3,2,1,0:T(8,128)S(1)}, u32[]{:S(2)}, u32[]{:S(2)}) collective-permute-start(f32[1,1,256,256]{3,2,1,0:T(8,128)S(1)} %get-tuple-element.205), channel_id=1, source_target_pairs={{1,0},{2,1},{3,2},{4,3},{5,4},{6,5},{7,6},{0,7},{9,8},{10,9},{11,1... | collective-permute-start | bytes 786440 | tf_op jit(solution)/shard_map/ppermute | solution.py:27
  82.3 11.1 collective-permute-start.5
  82.7 14.2 %collective-permute-start.4 = (f32[1,1,256,256]{3,2,1,0:T(8,128)S(1)}, f32[1,1,256,256]{3,2,1,0:T(8,128)S(1)}, u32[]{:S(2)}, u32[]{:S(2)}) collective-permute-start(f32[1,1,256,256]{3,2,1,0:T(8,128)S(1)} %get-tuple-element.195), channel_id=1, source_target_pairs={{1,0},{2,1},{3,2},{4,3},{5,4},{6,5},{7,6},{0,7},{9,8},{10,9},{11,1... | collective-permute-start | bytes 786440 | tf_op jit(solution)/shard_map/ppermute | solution.py:27
  93.4 117.5 %collective-permute-start.13 = (f32[1,1,64,64]{3,2,1,0:T(8,128)S(1)}, f32[1,1,64,64]{3,2,1,0:T(8,128)S(1)}, u32[]{:S(2)}, u32[]{:S(2)}) collective-permute-start(f32[1,1,64,64]{3,2,1,0:T(8,128)S(1)} %broadcast.258), channel_id=1, source_target_pairs={{0,1},{1,2},{2,3},{3,4},{4,5},{5,6},{6,7},{7,0},{8,9},{9,10},{10,1... | collective-permute-start | bytes 49160 | tf_op jit(solution)/shard_map/ppermute | solution.py:25
  284.7 11.5 %collective-permute-start.32 = (f32[1,1,256,256]{3,2,1,0:T(8,128)S(1)}, f32[1,1,256,256]{3,2,1,0:T(8,128)S(1)}, u32[]{:S(2)}, u32[]{:S(2)}) collective-permute-start(f32[1,1,256,256]{3,2,1,0:T(8,128)S(1)} %get-tuple-element.185), channel_id=1, source_target_pairs={{1,0},{2,1},{3,2},{4,3},{5,4},{6,5},{7,6},{0,7},{9,8},{10,9},{11,1... | collective-permute-start | bytes 786440 | tf_op jit(solution)/shard_map/ppermute | solution.py:27
  298.4 12.3 %collective-permute-start.34 = (f32[1,1,256,256]{3,2,1,0:T(8,128)S(1)}, f32[1,1,256,256]{3,2,1,0:T(8,128)S(1)}, u32[]{:S(2)}, u32[]{:S(2)}) collective-permute-start(f32[1,1,256,256]{3,2,1,0:T(8,128)S(1)} %get-tuple-element.175), channel_id=1, source_target_pairs={{1,0},{2,1},{3,2},{4,3},{5,4},{6,5},{7,6},{0,7},{9,8},{10,9},{11,1... | collective-permute-start | bytes 786440 | tf_op jit(solution)/shard_map/ppermute | solution.py:27
  313.1 13.8 %collective-permute-start.36 = (f32[1,1,256,256]{3,2,1,0:T(8,128)S(1)}, f32[1,1,256,256]{3,2,1,0:T(8,128)S(1)}, u32[]{:S(2)}, u32[]{:S(2)}) collective-permute-start(f32[1,1,256,256]{3,2,1,0:T(8,128)S(1)} %get-tuple-element.165), channel_id=1, source_target_pairs={{1,0},{2,1},{3,2},{4,3},{5,4},{6,5},{7,6},{0,7},{9,8},{10,9},{11,1... | collective-permute-start | bytes 786440 | tf_op jit(solution)/shard_map/ppermute | solution.py:27
  329.1 15.2 %collective-permute-start.38 = (f32[1,1,256,256]{3,2,1,0:T(8,128)S(1)}, f32[1,1,256,256]{3,2,1,0:T(8,128)S(1)}, u32[]{:S(2)}, u32[]{:S(2)}) collective-permute-start(f32[1,1,256,256]{3,2,1,0:T(8,128)S(1)} %get-tuple-element.155), channel_id=1, source_target_pairs={{1,0},{2,1},{3,2},{4,3},{5,4},{6,5},{7,6},{0,7},{9,8},{10,9},{11,1... | collective-permute-start | bytes 786440 | tf_op jit(solution)/shard_map/ppermute | solution.py:27
  619.1 13.1 %collective-permute-start.71 = (f32[1,1,256,256]{3,2,1,0:T(8,128)S(1)}, f32[1,1,256,256]{3,2,1,0:T(8,128)S(1)}, u32[]{:S(2)}, u32[]{:S(2)}) collective-permute-start(f32[1,1,256,256]{3,2,1,0:T(8,128)S(1)} %get-tuple-element.106), channel_id=1, source_target_pairs={{0,1},{1,2},{2,3},{3,4},{4,5},{5,6},{6,7},{7,0},{8,9},{9,10},{10,1... | collective-permute-start | bytes 786440 | tf_op jit(solution)/shard_map/ppermute | solution.py:25
  620.6 13.8 %collective-permute-start.70 = (f32[1,1,256,256]{3,2,1,0:T(8,128)S(1)}, f32[1,1,256,256]{3,2,1,0:T(8,128)S(1)}, u32[]{:S(2)}, u32[]{:S(2)}) collective-permute-start(f32[1,1,256,256]{3,2,1,0:T(8,128)S(1)} %get-tuple-element.105), channel_id=1, source_target_pairs={{1,0},{2,1},{3,2},{4,3},{5,4},{6,5},{7,6},{0,7},{9,8},{10,9},{11,1... | collective-permute-start | bytes 786440 | tf_op jit(solution)/shard_map/ppermute | solution.py:27
  636.5 11.1 collective-permute-start.73
  636.8 14.2 %collective-permute-start.72 = (f32[1,1,256,256]{3,2,1,0:T(8,128)S(1)}, f32[1,1,256,256]{3,2,1,0:T(8,128)S(1)}, u32[]{:S(2)}, u32[]{:S(2)}) collective-permute-start(f32[1,1,256,256]{3,2,1,0:T(8,128)S(1)} %get-tuple-element.95), channel_id=1, source_target_pairs={{1,0},{2,1},{3,2},{4,3},{5,4},{6,5},{7,6},{0,7},{9,8},{10,9},{11,1... | collective-permute-start | bytes 786440 | tf_op jit(solution)/shard_map/ppermute | solution.py:27
  851.0 13.0 %collective-permute-start.98 = (f32[1,1,256,256]{3,2,1,0:T(8,128)S(1)}, f32[1,1,256,256]{3,2,1,0:T(8,128)S(1)}, u32[]{:S(2)}, u32[]{:S(2)}) collective-permute-start(f32[1,1,256,256]{3,2,1,0:T(8,128)S(1)} %get-tuple-element.75), channel_id=1, source_target_pairs={{1,0},{2,1},{3,2},{4,3},{5,4},{6,5},{7,6},{0,7},{9,8},{10,9},{11,1... | collective-permute-start | bytes 786440 | tf_op jit(solution)/shard_map/ppermute | solution.py:27
  866.1 14.7 %collective-permute-start.100 = (f32[1,1,256,256]{3,2,1,0:T(8,128)S(1)}, f32[1,1,256,256]{3,2,1,0:T(8,128)S(1)}, u32[]{:S(2)}, u32[]{:S(2)}) collective-permute-start(f32[1,1,256,256]{3,2,1,0:T(8,128)S(1)} %get-tuple-element.65), channel_id=1, source_target_pairs={{1,0},{2,1},{3,2},{4,3},{5,4},{6,5},{7,6},{0,7},{9,8},{10,9},{11,1... | collective-permute-start | bytes 786440 | tf_op jit(solution)/shard_map/ppermute | solution.py:27
  883.0 11.2 collective-permute-start.103
  883.0 15.1 %collective-permute-start.102 = (f32[1,1,256,256]{3,2,1,0:T(8,128)S(1)}, f32[1,1,256,256]{3,2,1,0:T(8,128)S(1)}, u32[]{:S(2)}, u32[]{:S(2)}) collective-permute-start(f32[1,1,256,256]{3,2,1,0:T(8,128)S(1)} %get-tuple-element.55), channel_id=1, source_target_pairs={{1,0},{2,1},{3,2},{4,3},{5,4},{6,5},{7,6},{0,7},{9,8},{10,9},{11,1... | collective-permute-start | bytes 786440 | tf_op jit(solution)/shard_map/ppermute | solution.py:27
  (118 other events, 886.1 us)
Sparse Core Ops, SparseCore 0:
  26.2 34.4 all-gather.2
  579.9 34.7 all-gather.4
where the time goes:
time: 1140 us; the launch traced here: 1130 us
  waiting for transfers between devices  381 us (33%)
  local copies, waits for them, and re-layouts  337 us (30%)
  starting transfers between devices  252 us (22%)
  other arithmetic  140 us (12%)
  between operations  19.1 us (2%)
    reshape x4, local copies, waits for them, and re-layouts, restrict(): field.reshape(a, b // 2, 2, c // 2, 2, d // 2, 2).mean(axis=(2, 4, 6))  274 us
    ppermute x66, waiting for transfers between devices, extended(): lax.ppermute(tail, axis, [(i, (i + 1) % count) for i in range(count)])  226 us
    ppermute x66, starting transfers between devices, extended(): lax.ppermute(head, axis, [((i + 1) % count, i) for i in range(count)])  187 us
    reduce_sum x12, other arithmetic, restrict(): field.reshape(a, b // 2, 2, c // 2, 2, d // 2, 2).mean(axis=(2, 4, 6))  94.9 us
    ppermute x66, waiting for transfers between devices, extended(): lax.ppermute(head, axis, [((i + 1) % count, i) for i in range(count)])  94.8 us
    ppermute x66, starting transfers between devices, extended(): lax.ppermute(tail, axis, [(i, (i + 1) % count) for i in range(count)])  64.8 us
    all_gather x2, waiting for transfers between devices, per_device(): piece = lax.all_gather(force, 'node', axis=0, tiled=True)  59.5 us
    add x56, other arithmetic, smooth(): return field + OMEGA * (source - applied) / (1.0 + 6.0 * shift)  28.4 us
  transfers between devices with their start and end apart: 134, of which 114 were waited for; matrix products, arithmetic and copies ran while one was open for 10% of the time, Pallas kernels for 0%

commit v1 on v0

v1 whole, which is shorter than its diff:
```python
import functools

import jax
import jax.numpy as jnp
from jax import lax
from jax.experimental import pallas as pl
from jax.experimental.pallas import tpu as pltpu
from jax.sharding import PartitionSpec as P

SWEEPS = 2
VCYCLES = 2
COARSE = 8

DIFFUSE = 2.0
REACT = 0.5
OMEGA = 0.8

HALO = 4
EXACT = lax.Precision.HIGHEST


def radau_gap(count, where):
    previous = 1.0
    current = where
    for degree in range(1, count):
        following = ((2 * degree + 1) * where * current - degree * previous) / (degree + 1)
        previous = current
        current = following
    return current - previous


def radau_table(count):
    zeros_found = []
    grid_count = 4096
    lower = -1.0
    value_low = radau_gap(count, lower)
    for place in range(1, grid_count):
        upper = -1.0 + 2.0 * place / grid_count
        value_up = radau_gap(count, upper)
        if value_low * value_up < 0.0:
            left_end = lower
            right_end = upper
            left_value = value_low
            for halving in range(100):
                middle = 0.5 * (left_end + right_end)
                middle_value = radau_gap(count, middle)
                if left_value * middle_value <= 0.0:
                    right_end = middle
                else:
                    left_end = middle
                    left_value = middle_value
            zeros_found.append(0.5 * (left_end + right_end))
        lower = upper
        value_low = value_up
    zeros_found.append(1.0)
    abscissa = [(value + 1.0) / 2.0 for value in zeros_found]
    table_rows = []
    for outer in range(count):
        table_rows.append([0.0] * count)
    for column in range(count):
        factor = [1.0]
        scale = 1.0
        for other in range(count):
            if other != column:
                widened = [0.0] * (len(factor) + 1)
                for power in range(len(factor)):
                    widened[power + 1] = widened[power + 1] + factor[power]
                    widened[power] = widened[power] - abscissa[other] * factor[power]
                factor = widened
                scale = scale * (abscissa[column] - abscissa[other])
        for outer in range(count):
            upto = abscissa[outer]
            accum = 0.0
            for power in range(len(factor)):
                accum = accum + factor[power] * upto ** (power + 1) / (power + 1)
            table_rows[outer][column] = accum / scale
    return (abscissa, table_rows)


def ring_order(count):
    return list(range(0, count, 2)) + list(range(count - 1 - count % 2, 0, -2))


def rows_loop(count, body):
    step = next(k for k in (4, 3, 2, 1) if count % k == 0)

    def some(i, carry):
        for k in range(step):
            body(i * step + k)
        return carry

    lax.fori_loop(0, count // step, some, 0)


def six(ref, row):
    here = ref[row]
    tall, wide = here.shape
    total = ref[row - 1] + ref[row + 1]
    total = total + (pltpu.roll(here, 1, 0) + pltpu.roll(here, tall - 1, 0))
    total = total + (pltpu.roll(here, 1, 1) + pltpu.roll(here, wide - 1, 1))
    return here, total


def sweep(src, src_at, source, source_at, dst, dst_at, count, shift):
    weight = OMEGA / (1.0 + 6.0 * shift)
    spread = weight * shift

    def body(row):
        here, total = six(src, row + src_at)
        dst[row + dst_at] = (1.0 - OMEGA) * here + weight * source[row + source_at] + spread * total

    rows_loop(count, body)


def residual(src, src_at, source, source_at, row, shift):
    here, total = six(src, row + src_at)
    return source[row + source_at] - (1.0 + 6.0 * shift) * here + shift * total


def copy_rows(src, src_at, dst, dst_at, count):
    def body(row):
        dst[row + dst_at] = src[row + src_at]

    rows_loop(count, body)


def force_kernel(shift_ref, lo, mid, hi, first, kappa, force, base, wide):
    shift = shift_ref[0]
    count = mid.shape[0]
    copy_rows(lo, 0, wide, 0, HALO)
    copy_rows(mid, 0, wide, HALO, count)
    copy_rows(hi, 0, wide, HALO + count, HALO)

    def body(row):
        here, total = six(wide, row + 1)
        lap = total - 6.0 * here
        strength = kappa[row + 1]
        force[row] = DIFFUSE * lap + REACT * strength * (here - here * here * here)
        base[row] = first[row + 1] - shift * lap

    rows_loop(count + 2 * HALO - 2, body)


def before_kernel(shift_ref, lo, mid, hi, right, squeeze, field, source1, wide, other, summed, thin):
    shift = shift_ref[0]
    count = mid.shape[0]
    copy_rows(lo, 0, wide, 0, HALO)
    copy_rows(mid, 0, wide, HALO, count)
    copy_rows(hi, 0, wide, HALO + count, HALO)
    sweep(wide, 1, right, 0, other, 0, count + 6, shift)
    sweep(other, 1, right, 1, field, 0, count + 4, shift)

    def body(row):
        at = 2 * row
        summed[row] = residual(field, at + 2, right, at + 3, 0, shift) + residual(
            field, at + 3, right, at + 4, 0, shift
        )

    rows_loop(count // 2, body)
    half, tall, across = summed.shape
    thin[...] = jnp.dot(summed[...].reshape(half * tall, across), squeeze[...], precision=EXACT).reshape(thin.shape)
    source1[...] = thin[:, pl.ds(0, tall // 2, stride=2), :] + thin[:, pl.ds(1, tall // 2, stride=2), :]


def middle_kernel(shift_ref, lo, mid, hi, squeeze, field1, wide1, source2, first, summed):
    shift = shift_ref[0] / 4.0
    count = mid.shape[0]
    copy_rows(lo, 0, wide1, 0, HALO)
    copy_rows(mid, 0, wide1, HALO, count)
    copy_rows(hi, 0, wide1, HALO + count, HALO)
    weight = OMEGA / (1.0 + 6.0 * shift)

    def start(row):
        first[row] = weight * wide1[row]

    rows_loop(count + 2 * HALO, start)
    sweep(first, 1, wide1, 1, field1, 0, count + 6, shift)

    def body(row):
        at = 2 * row
        summed[row] = residual(field1, at + 3, wide1, at + 4, 0, shift) + residual(
            field1, at + 4, wide1, at + 5, 0, shift
        )

    rows_loop(count // 2, body)
    half, tall, across = summed.shape
    short = summed[:, pl.ds(0, tall // 2, stride=2), :] + summed[:, pl.ds(1, tall // 2, stride=2), :]
    short = short.reshape(half * tall // 2, across)
    source2[...] = jnp.dot(short, squeeze[...], precision=EXACT).reshape(source2.shape)


def after_kernel(
    order, shift_ref, place, parts, field1, wide1, field, right, stretch2, stretch1, out,
    source2, even, odd, error2, work1, more1, error1, work, more, last,
):
    shift = shift_ref[0]
    shift1 = shift / 4.0
    shift2 = shift1 / 4.0
    devices, own = parts.shape[:2]
    rows = devices * own
    for at, device in enumerate(order):
        source2[pl.ds(at * own, own)] = parts[device]
    weight = OMEGA / (1.0 + 6.0 * shift2)

    def start(row):
        even[row + 1] = weight * source2[row]

    rows_loop(rows, start)
    here, there = even, odd
    for step in range(COARSE - 1):
        here[0] = here[rows]
        here[rows + 1] = here[1]
        sweep(here, 1, source2, 0, there, 1, rows, shift2)
        here, there = there, here
    begin = place[0] * own

    def pick(row):
        error2[row] = here[lax.rem(begin + row - 2 + rows, rows) + 1]

    rows_loop(own + 4, pick)
    tall2 = error2.shape[1]
    spread = jnp.dot(
        error2[...].reshape((own + 4) * tall2, error2.shape[2]), stretch2[...], precision=EXACT
    ).reshape(own + 4, tall2, stretch2.shape[1])
    tall1 = 2 * tall2
    work1[:, pl.ds(0, tall2, stride=2), :] = spread
    work1[:, pl.ds(1, tall2, stride=2), :] = spread
    count1 = 2 * own

    def correct1(row):
        more1[row] = field1[row] + work1[(row + 1) // 2]

    rows_loop(count1 + 6, correct1)
    sweep(more1, 1, wide1, 2, error1, 0, count1 + 4, shift1)
    sweep(error1, 1, wide1, 3, more1, 0, count1 + 2, shift1)
    tall = 2 * tall1
    half = more1[pl.ds(0, count1 + 2)]
    work[:, pl.ds(0, tall1, stride=2), :] = half
    work[:, pl.ds(1, tall1, stride=2), :] = half
    count = 2 * count1

    def correct(row):
        fine = jnp.dot(work[row], stretch1[...], precision=EXACT)
        more[2 * row] = field[2 * row] + fine
        more[2 * row + 1] = field[2 * row + 1] + fine

    rows_loop(count1 + 2, correct)
    sweep(more, 1, right, 2, last, 0, count + 2, shift)
    sweep(last, 1, right, 3, out, 0, count, shift)


def call(kernel, outs, scratch, *args):
    specs = [pl.BlockSpec(memory_space=pltpu.SMEM if a.ndim == 1 else pltpu.VMEM) for a in args]
    return pl.pallas_call(
        kernel,
        out_shape=[jax.ShapeDtypeStruct(shape, jnp.float32) for shape in outs],
        in_specs=specs,
        out_specs=[pl.BlockSpec(memory_space=pltpu.VMEM)] * len(outs),
        scratch_shapes=[pltpu.VMEM(shape, jnp.float32) for shape in scratch],
        compiler_params=pltpu.CompilerParams(vmem_limit_bytes=60 * 2**20),
    )(*args)


def pairing(fine, coarse, value):
    lanes = jnp.arange(coarse)[None, :] % (fine // 2)
    return jnp.where(jnp.arange(fine)[:, None] // 2 == lanes, value, 0.0).astype(jnp.float32)


def per_device(initial, kappa):
    nodes = lax.axis_size("node")
    position = lax.axis_index("node")
    devices = lax.axis_size("space")
    order = ring_order(devices)
    rank = [order.index(device) for device in range(devices)]
    place = jnp.asarray(rank, jnp.int32)[lax.axis_index("space")][None]
    up = [(order[i], order[(i + 1) % devices]) for i in range(devices)]
    down = [(target, source) for source, target in up]
    across = [(i, i ^ 1) for i in range(nodes)]
    abscissa, table_rows = radau_table(nodes)
    table = jnp.asarray(table_rows, jnp.float32)
    shift = jnp.asarray([DIFFUSE * value for value in abscissa], jnp.float32)[position]
    params = shift[None]

    planes, rows, cells = initial.shape
    tall = planes * devices
    own = rows // devices
    own1, tall1, cells1 = own // 2, tall // 2, cells // 2
    own2, tall2, cells2 = own // 4, tall // 4, max(128, cells // 4)
    squeeze = pairing(cells, cells1, 0.125)
    squeeze1 = pairing(cells1, cells2, 0.125)
    stretch1 = pairing(cells, cells1, 1.0).T
    stretch2 = jnp.where(jnp.arange(cells2)[None, :] < cells1 // 2, pairing(cells1, cells2, 1.0), 0.0).T

    def halo(mid):
        lo = lax.ppermute(mid[-HALO:], "space", up)
        hi = lax.ppermute(mid[:HALO], "space", down)
        return lo, mid, hi

    def spread_out(field):
        pieces = field.reshape(planes, devices, own, cells).transpose(1, 2, 0, 3)
        pieces = jnp.stack([pieces[at] for at in rank])
        pieces = lax.all_to_all(pieces, "space", 0, 0)
        return pieces.transpose(1, 0, 2, 3).reshape(own, tall, cells)

    def bring_back(field):
        pieces = field.reshape(own, devices, planes, cells).transpose(1, 2, 0, 3)
        pieces = lax.all_to_all(pieces, "space", 0, 0)
        pieces = jnp.stack([pieces[device] for device in order])
        return pieces.transpose(1, 0, 2, 3).reshape(planes, rows, cells)

    first_core = position % 2 == 0
    mine = jnp.concatenate(halo(spread_out(jnp.where(first_core, initial, kappa))))
    others = lax.ppermute(mine, "node", across)
    first = jnp.where(first_core, mine, others)
    strength = jnp.where(first_core, others, mine)
    parts = (first[:HALO], first[HALO:-HALO], first[-HALO:])

    extra = own + 2 * HALO
    for step in range(SWEEPS):
        force, base = call(
            force_kernel,
            [(extra - 2, tall, cells)] * 2,
            [(extra, tall, cells)],
            params, *parts, first, strength,
        )
        if step == 0:
            right = base + jnp.sum(table[position]) * force
        else:
            right = base
            held = force
            for turn in range(nodes // 2):
                if turn:
                    held = lax.ppermute(force, "node", [(i, (i + 2 * turn) % nodes) for i in range(nodes)])
                origin = (position - 2 * turn) % nodes
                beside = lax.ppermute(held, "node", across)
                right = right + table[position, origin] * held + table[position, origin ^ 1] * beside
        for cycle in range(VCYCLES):
            field, source1 = call(
                before_kernel,
                [(own + 4, tall, cells), (own1, tall1, cells1)],
                [(extra, tall, cells), (own + 6, tall, cells), (own1, tall, cells), (own1, tall, cells1)],
                params, *parts, right, squeeze,
            )
            field1, wide1, source2 = call(
                middle_kernel,
                [(own1 + 6, tall1, cells1), (own1 + 8, tall1, cells1), (own2, tall2, cells2)],
                [(own1 + 8, tall1, cells1), (own2, tall1, cells1)],
                params, *halo(source1), squeeze1,
            )
            pieces = lax.all_gather(source2, "space")
            (section,) = call(
                functools.partial(after_kernel, order),
                [(own, tall, cells)],
                [
                    (own2 * devices, tall2, cells2),
                    (own2 * devices + 2, tall2, cells2),
                    (own2 * devices + 2, tall2, cells2),
                    (own2 + 4, tall2, cells2),
                    (own2 + 4, tall1, cells1),
                    (own1 + 6, tall1, cells1),
                    (own1 + 4, tall1, cells1),
                    (own1 + 2, tall, cells1),
                    (own + 4, tall, cells),
                    (own + 2, tall, cells),
                ],
                params, place, pieces, field1, wide1, field, right, stretch2, stretch1,
            )
            if step + 1 < SWEEPS or cycle + 1 < VCYCLES:
                parts = halo(section)
    return bring_back(section)[None]


def solution(mesh):
    in_specs = (P("space", None, None), P("space", None, None))
    out_specs = P("node", "space", None, None)
    return jax.shard_map(
        per_device, mesh=mesh, in_specs=in_specs, out_specs=out_specs, check_vma=False
    )
```

time: 1140 us -> 418 us (0.37)
  waiting for transfers between devices: 381 us -> 38.6 us
  local copies, waits for them, and re-layouts: 337 us -> 22.4 us
  starting transfers between devices: 252 us -> 18 us
  blocking collectives: 0 us -> 184 us
  Pallas kernels: 0 us -> 136 us
  other arithmetic: 140 us -> 16.9 us
  between operations: 19.1 us -> 0.33 us
    ppermute x132 -> x20, waiting for transfers between devices: 321 us -> 38.6 us  [the longest x8 16.8 us: halo(): hi = lax.ppermute(mid[:HALO], 'space', down)]
    reshape x4 -> x3, local copies, waits for them, and re-layouts: 274 us -> 2.08 us  [the longest x2 1.72 us: bring_back(): pieces = field.reshape(own, devices, planes, cells).transpose(1, 2, 0, 3)]
    ppermute x132 -> x20, starting transfers between devices: 252 us -> 18 us  [the longest x8 14.3 us: halo(): lo = lax.ppermute(mid[-HALO:], 'space', up)]
    pallas_call x0 -> x14, Pallas kernels: none -> 136 us  [call(): pl.pallas_call(kernel, out_shape=[jax.ShapeDtypeStruct(shape, jnp.float32...]
    all_gather x0 -> x4, blocking collectives: none -> 132 us  [per_device(): pieces = lax.all_gather(source2, 'space')]
    reduce_sum x14 -> x1, other arithmetic: 100 us -> 0.66 us  [per_device(): right = base + jnp.sum(table[position]) * force]
    all_gather x2 -> x0, waiting for transfers between devices: 59.5 us -> none  [per_device(): piece = lax.all_gather(force, 'node', axis=0, tiled=True)]
    all_to_all x0 -> x2, blocking collectives: none -> 52.2 us  [the longest x1 32.9 us: spread_out(): pieces = lax.all_to_all(pieces, 'space', 0, 0)]
  transfers between devices with their start and end apart: 134 -> 20, of which waited for: 114 -> 19; matrix products, arithmetic and copies ran while one was open for 10% -> 1% of each run, Pallas kernels for 0% -> 0%
where the time goes in v1:
time: 418 us; the launch traced here: 416 us
  blocking collectives  184 us (44%)
  Pallas kernels  136 us (33%)
  waiting for transfers between devices  38.6 us (9%)
  local copies, waits for them, and re-layouts  22.4 us (5%)
  starting transfers between devices  18 us (4%)
  other arithmetic  16.9 us (4%)
    pallas_call x14, Pallas kernels, call(): pl.pallas_call(kernel, out_shape=[jax.ShapeDtypeStruct(shape, jnp.float32...  136 us
    all_gather x4, blocking collectives, per_device(): pieces = lax.all_gather(source2, 'space')  132 us
    all_to_all x1, blocking collectives, spread_out(): pieces = lax.all_to_all(pieces, 'space', 0, 0)  32.9 us
    all_to_all x1, blocking collectives, bring_back(): pieces = lax.all_to_all(pieces, 'space', 0, 0)  19.3 us
    ppermute x8, waiting for transfers between devices, halo(): hi = lax.ppermute(mid[:HALO], 'space', down)  16.8 us
    ppermute x1, waiting for transfers between devices, per_device(): lax.ppermute(force, 'node', [(i, (i + 2 * turn) % nodes) for i in range(n...  15.6 us
    ppermute x8, starting transfers between devices, halo(): lo = lax.ppermute(mid[-HALO:], 'space', up)  14.3 us
  transfers between devices with their start and end apart: 20, of which 19 were waited for; matrix products, arithmetic and copies ran while one was open for 1% of the time, Pallas kernels for 0%

profile of v1, /device:TPU:0, one launch (start us, length us, event | category | flops | bytes accessed | tf_op | source)
XLA Modules:
  0.0 416.3 jit_solution(7833244130035478887)
XLA Ops:
  2.3 32.9 %all_to_all.10 = f32[8,32,4,256]{3,2,1,0:T(4,128)S(1)} all-to-all(f32[8,32,4,256]{3,2,1,0:T(4,128)S(1)} %slice_dynamic-update-slice_fusion.1), channel_id=1, replica_groups=mesh['node'=4,'space'=8] {'space'}, dimensions={0} | all-to-all | bytes 2097152 | tf_op jit(solution)/shard_map/all_to_all | solution.py:302
  49.9 6.4 %shard_map.55 = (f32[38,32,256]{2,1,0:T(8,128)}, f32[38,32,256]{2,1,0:T(8,128)}) custom-call(f32[1]{0:T(128)} %dynamic_slice.21.shift_ref, f32[4,32,256]{2,1,0:T(8,128)} %get-tuple-element.56.lo, f32[32,32,256]{2,1,0:T(8,128)} %slice.154.mid, f32[4,32,256]{2,1,0:T(8,128)} %get-tuple-element.55.hi, f32[40,32,256]{2,1,0:T(8,128)} %copy-done, ...), custom_call_target="tpu_custom_call" | custom-call | tf_op jit(solution)/shard_map/pallas_call | solution.py:254
  56.3 3.6 multiply_add_fusion.1.right
  59.9 7.9 %shard_map.56 = (f32[36,32,256]{2,1,0:T(8,128)}, f32[16,16,128]{2,1,0:T(8,128)}) custom-call(f32[1]{0:T(128)} %dynamic_slice.21.shift_ref, f32[4,32,256]{2,1,0:T(8,128)} %get-tuple-element.56.lo, f32[32,32,256]{2,1,0:T(8,128)} %slice.154.mid, f32[4,32,256]{2,1,0:T(8,128)} %get-tuple-element.55.hi, f32[38,32,256]{2,1,0:T(8,128)} %multiply_add_fusion.1.right, ...), custom_call_target="tpu_custom_call" | custom-call | tf_op jit(solution)/shard_map/pallas_call | solution.py:254
  74.1 3.5 shard_map.57
  77.6 32.9 %all-gather = f32[64,8,128]{2,1,0:T(8,128)} all-gather(f32[8,8,128]{2,1,0:T(8,128)} %get-tuple-element.32), channel_id=2, replica_groups=mesh['node'=4,'space'=8] {'space'}, dimensions={0}, use_global_device_ids=true | all-gather | bytes 294912 | tf_op jit(solution)/shard_map/all_gather | solution.py:350
  110.6 19.4 %shard_map.58.mid = f32[32,32,256]{2,1,0:T(8,128)} custom-call(f32[1]{0:T(128)} %dynamic_slice.21.shift_ref, s32[1]{0:T(128)} %dynamic_slice.22.place, f32[8,8,8,128]{3,2,1,0:T(8,128)} %bitcast.30, f32[22,16,128]{2,1,0:T(8,128)} %get-tuple-element.33.field1, f32[24,16,128]{2,1,0:T(8,128)} %get-tuple-element.34.wide1, ...), custom_call_target="tpu_custom_call" | custom-call | tf_op jit(solution)/shard_map/pallas_call | solution.py:254
  133.0 2.9 collective-permute-done.6.hi
  137.2 7.8 %shard_map.59 = (f32[36,32,256]{2,1,0:T(8,128)}, f32[16,16,128]{2,1,0:T(8,128)}) custom-call(f32[1]{0:T(128)} %dynamic_slice.21.shift_ref, f32[4,32,256]{2,1,0:T(8,128)} %copy-done.6, f32[32,32,256]{2,1,0:T(8,128)} %shard_map.58.mid, f32[4,32,256]{2,1,0:T(8,128)} %copy-done.4, f32[38,32,256]{2,1,0:T(8,128)} %multiply_add_fusion.1.right, ...), custom_call_target="tpu_custom_call" | custom-call | tf_op jit(solution)/shard_map/pallas_call | solution.py:254
  151.0 3.5 shard_map.60
  154.6 32.9 %all-gather.1 = f32[64,8,128]{2,1,0:T(8,128)} all-gather(f32[8,8,128]{2,1,0:T(8,128)} %get-tuple-element.37), channel_id=3, replica_groups=mesh['node'=4,'space'=8] {'space'}, dimensions={0}, use_global_device_ids=true | all-gather | bytes 294912 | tf_op jit(solution)/shard_map/all_gather | solution.py:350
  187.5 19.4 %shard_map.61.mid = f32[32,32,256]{2,1,0:T(8,128)} custom-call(f32[1]{0:T(128)} %dynamic_slice.21.shift_ref, s32[1]{0:T(128)} %dynamic_slice.22.place, f32[8,8,8,128]{3,2,1,0:T(8,128)} %bitcast.31, f32[22,16,128]{2,1,0:T(8,128)} %get-tuple-element.38.field1, f32[24,16,128]{2,1,0:T(8,128)} %get-tuple-element.39.wide1, ...), custom_call_target="tpu_custom_call" | custom-call | tf_op jit(solution)/shard_map/pallas_call | solution.py:254
  214.2 6.4 %shard_map.62 = (f32[38,32,256]{2,1,0:T(8,128)}, f32[38,32,256]{2,1,0:T(8,128)}) custom-call(f32[1]{0:T(128)} %dynamic_slice.21.shift_ref, f32[4,32,256]{2,1,0:T(8,128)} %copy-done.2, f32[32,32,256]{2,1,0:T(8,128)} %shard_map.61.mid, f32[4,32,256]{2,1,0:T(8,128)} %copy-done.1, f32[40,32,256]{2,1,0:T(8,128)} %copy-done, f32[40,32,256]{2,1,0:T(8,128)} %get-tuple-element.53.kappa), custom_call_target="tpu_custom_call" | custom-call | tf_op jit(solution)/shard_map/pallas_call | solution.py:254
  222.1 15.6 %collective-permute-done.12 = f32[38,32,256]{2,1,0:T(8,128)S(1)} collective-permute-done((f32[38,32,256]{2,1,0:T(8,128)}, f32[38,32,256]{2,1,0:T(8,128)S(1)}, u32[]{:S(2)}, u32[]{:S(2)}) %collective-permute-start.12) | collective-permute-done | bytes 1245216 | tf_op jit(solution)/shard_map/ppermute | solution.py:333
  240.8 6.4 %multiply_add_fusion.right = f32[38,32,256]{2,1,0:T(8,128)} fusion(f32[38,32,256]{2,1,0:T(8,128)} %collective-permute-done.13, f32[38,32,256]{2,1,0:T(8,128)S(1)} %collective-permute-done.12, f32[38,32,256]{2,1,0:T(8,128)S(1)} %collective-permute-done.11, f32[38,32,256]{2,1,0:T(8,128)} %get-tuple-element.41, f32[38,32,256]{2,1,0:T(8,128)} %get-tuple-element.42, ...), kind=kLoop, calls=%fused_computation | loop fusion | flops 2490368 | bytes 7471120 | tf_op jit(solution)/shard_map/add | solution.py:336
  247.2 7.9 %shard_map.63 = (f32[36,32,256]{2,1,0:T(8,128)}, f32[16,16,128]{2,1,0:T(8,128)}) custom-call(f32[1]{0:T(128)} %dynamic_slice.21.shift_ref, f32[4,32,256]{2,1,0:T(8,128)} %copy-done.2, f32[32,32,256]{2,1,0:T(8,128)} %shard_map.61.mid, f32[4,32,256]{2,1,0:T(8,128)} %copy-done.1, f32[38,32,256]{2,1,0:T(8,128)} %multiply_add_fusion.right, ...), custom_call_target="tpu_custom_call" | custom-call | tf_op jit(solution)/shard_map/pallas_call | solution.py:254
  260.9 3.5 shard_map.64
  264.5 33.1 %all-gather.2 = f32[64,8,128]{2,1,0:T(8,128)} all-gather(f32[8,8,128]{2,1,0:T(8,128)} %get-tuple-element.44), channel_id=4, replica_groups=mesh['node'=4,'space'=8] {'space'}, dimensions={0}, use_global_device_ids=true | all-gather | bytes 294912 | tf_op jit(solution)/shard_map/all_gather | solution.py:350
  297.6 19.4 %shard_map.65.mid = f32[32,32,256]{2,1,0:T(8,128)} custom-call(f32[1]{0:T(128)} %dynamic_slice.21.shift_ref, s32[1]{0:T(128)} %dynamic_slice.22.place, f32[8,8,8,128]{3,2,1,0:T(8,128)} %bitcast.32, f32[22,16,128]{2,1,0:T(8,128)} %get-tuple-element.45.field1, f32[24,16,128]{2,1,0:T(8,128)} %get-tuple-element.46.wide1, ...), custom_call_target="tpu_custom_call" | custom-call | tf_op jit(solution)/shard_map/pallas_call | solution.py:254
  324.3 7.9 %shard_map.66 = (f32[36,32,256]{2,1,0:T(8,128)}, f32[16,16,128]{2,1,0:T(8,128)}) custom-call(f32[1]{0:T(128)} %dynamic_slice.21.shift_ref, f32[4,32,256]{2,1,0:T(8,128)} %copy-done.5, f32[32,32,256]{2,1,0:T(8,128)} %shard_map.65.mid, f32[4,32,256]{2,1,0:T(8,128)} %copy-done.3, f32[38,32,256]{2,1,0:T(8,128)} %multiply_add_fusion.right, ...), custom_call_target="tpu_custom_call" | custom-call | tf_op jit(solution)/shard_map/pallas_call | solution.py:254
  338.1 3.5 shard_map.67
  341.6 32.9 %all-gather.3 = f32[64,8,128]{2,1,0:T(8,128)} all-gather(f32[8,8,128]{2,1,0:T(8,128)} %get-tuple-element.49), channel_id=5, replica_groups=mesh['node'=4,'space'=8] {'space'}, dimensions={0}, use_global_device_ids=true | all-gather | bytes 294912 | tf_op jit(solution)/shard_map/all_gather | solution.py:350
  374.5 19.4 %shard_map.68 = f32[32,32,256]{2,1,0:T(8,128)} custom-call(f32[1]{0:T(128)} %dynamic_slice.21.shift_ref, s32[1]{0:T(128)} %dynamic_slice.22.place, f32[8,8,8,128]{3,2,1,0:T(8,128)} %bitcast.29, f32[22,16,128]{2,1,0:T(8,128)} %get-tuple-element.50.field1, f32[24,16,128]{2,1,0:T(8,128)} %get-tuple-element.51.wide1, f32[36,32,256]{2,1,0:T(8,128)} %get-tuple-element.52.field, ...), custom_call_target="tpu_custom_call" | custom-call | tf_op jit(solution)/shard_map/pallas_call | solution.py:254
  395.6 19.3 %all_to_all.11 = f32[8,4,32,256]{3,1,2,0:T(4,128)S(1)} all-to-all(f32[8,4,32,256]{3,1,2,0:T(4,128)S(1)} %bitcast.27), channel_id=1, replica_groups=mesh['node'=4,'space'=8] {'space'}, dimensions={0} | all-to-all | bytes 2097152 | tf_op jit(solution)/shard_map/all_to_all | solution.py:307
  (124 shorter events, 67.4 us)
Async XLA Ops:
  35.2 5.0 %collective-permute-start = (f32[4,32,256]{2,1,0:T(8,128)S(1)}, f32[4,32,256]{2,1,0:T(8,128)S(1)}, u32[]{:S(2)}, u32[]{:S(2)}) collective-permute-start(f32[4,32,256]{2,1,0:T(8,128)S(1)} %slice.117), channel_id=1, source_target_pairs={{0,2},{2,4},{4,6},{6,7},{7,5},{5,3},{3,1},{1,0},{8,10},{10,12},{12... | collective-permute-start | bytes 393224 | tf_op jit(solution)/shard_map/ppermute | solution.py:295
  37.1 5.0 %collective-permute-start.1 = (f32[4,32,256]{2,1,0:T(8,128)S(1)}, f32[4,32,256]{2,1,0:T(8,128)S(1)}, u32[]{:S(2)}, u32[]{:S(2)}) collective-permute-start(f32[4,32,256]{2,1,0:T(8,128)S(1)} %slice.119), channel_id=1, source_target_pairs={{2,0},{4,2},{6,4},{7,6},{5,7},{3,5},{1,3},{0,1},{10,8},{12,10},{14... | collective-permute-start | bytes 393224 | tf_op jit(solution)/shard_map/ppermute | solution.py:296
  40.2 1.9 copy-start.15
  40.3 2.6 copy-start.17
  42.1 3.2 collective-permute-start.2
  48.0 1.9 copy-start
  59.9 11.4 %copy-start.16 = (s32[8]{0:T(128)S(1)}, s32[8]{0:T(128)}, u32[]{:S(2)}) copy-start(s32[8]{0:T(128)} %constant.115.clone) | copy-start | bytes 100
  68.6 3.9 collective-permute-start.4
  69.5 3.9 collective-permute-start.3
  130.9 5.0 %collective-permute-start.6 = (f32[4,32,256]{2,1,0:T(8,128)S(1)}, f32[4,32,256]{2,1,0:T(8,128)S(1)}, u32[]{:S(2)}, u32[]{:S(2)}) collective-permute-start(f32[4,32,256]{2,1,0:T(8,128)S(1)} %get-tuple-element.61), channel_id=1, source_target_pairs={{2,0},{4,2},{6,4},{7,6},{5,7},{3,5},{1,3},{0,1},{10,8},{12,10},{14... | collective-permute-start | bytes 393224 | tf_op jit(solution)/shard_map/ppermute | solution.py:296
  131.0 5.0 %collective-permute-start.5 = (f32[4,32,256]{2,1,0:T(8,128)S(1)}, f32[4,32,256]{2,1,0:T(8,128)S(1)}, u32[]{:S(2)}, u32[]{:S(2)}) collective-permute-start(f32[4,32,256]{2,1,0:T(8,128)S(1)} %get-tuple-element.62), channel_id=1, source_target_pairs={{0,2},{2,4},{4,6},{6,7},{7,5},{5,3},{3,1},{1,0},{8,10},{10,12},{12... | collective-permute-start | bytes 393224 | tf_op jit(solution)/shard_map/ppermute | solution.py:295
  145.9 3.9 collective-permute-start.8
  145.9 4.0 collective-permute-start.7
  207.9 5.0 %collective-permute-start.10 = (f32[4,32,256]{2,1,0:T(8,128)S(1)}, f32[4,32,256]{2,1,0:T(8,128)S(1)}, u32[]{:S(2)}, u32[]{:S(2)}) collective-permute-start(f32[4,32,256]{2,1,0:T(8,128)S(1)} %get-tuple-element.59), channel_id=1, source_target_pairs={{2,0},{4,2},{6,4},{7,6},{5,7},{3,5},{1,3},{0,1},{10,8},{12,10},{14... | collective-permute-start | bytes 393224 | tf_op jit(solution)/shard_map/ppermute | solution.py:296
  207.9 5.0 %collective-permute-start.9 = (f32[4,32,256]{2,1,0:T(8,128)S(1)}, f32[4,32,256]{2,1,0:T(8,128)S(1)}, u32[]{:S(2)}, u32[]{:S(2)}) collective-permute-start(f32[4,32,256]{2,1,0:T(8,128)S(1)} %get-tuple-element.60), channel_id=1, source_target_pairs={{0,2},{2,4},{4,6},{6,7},{7,5},{5,3},{3,1},{1,0},{8,10},{10,12},{12... | collective-permute-start | bytes 393224 | tf_op jit(solution)/shard_map/ppermute | solution.py:295
  220.6 17.1 %collective-permute-start.12 = (f32[38,32,256]{2,1,0:T(8,128)}, f32[38,32,256]{2,1,0:T(8,128)S(1)}, u32[]{:S(2)}, u32[]{:S(2)}) collective-permute-start(f32[38,32,256]{2,1,0:T(8,128)} %get-tuple-element.42), channel_id=1, source_target_pairs={{0,16},{8,24},{16,0},{24,8},{1,17},{9,25},{17,1},{25,9},{2,18},{10... | collective-permute-start | bytes 3735560 | tf_op jit(solution)/shard_map/ppermute | solution.py:333
  222.1 16.3 %collective-permute-start.11 = (f32[38,32,256]{2,1,0:T(8,128)}, f32[38,32,256]{2,1,0:T(8,128)S(1)}, u32[]{:S(2)}, u32[]{:S(2)}) collective-permute-start(f32[38,32,256]{2,1,0:T(8,128)} %get-tuple-element.42), channel_id=1, source_target_pairs={{0,8},{8,0},{16,24},{24,16},{1,9},{9,1},{17,25},{25,17},{2,10},{10... | collective-permute-start | bytes 3735560 | tf_op jit(solution)/shard_map/ppermute | solution.py:335
  237.7 3.1 collective-permute-start.13
  255.8 3.9 collective-permute-start.15
  255.8 4.0 collective-permute-start.14
  317.9 5.0 %collective-permute-start.17 = (f32[4,32,256]{2,1,0:T(8,128)S(1)}, f32[4,32,256]{2,1,0:T(8,128)S(1)}, u32[]{:S(2)}, u32[]{:S(2)}) collective-permute-start(f32[4,32,256]{2,1,0:T(8,128)S(1)} %get-tuple-element.57), channel_id=1, source_target_pairs={{2,0},{4,2},{6,4},{7,6},{5,7},{3,5},{1,3},{0,1},{10,8},{12,10},{14... | collective-permute-start | bytes 393224 | tf_op jit(solution)/shard_map/ppermute | solution.py:296
  318.0 5.0 %collective-permute-start.16 = (f32[4,32,256]{2,1,0:T(8,128)S(1)}, f32[4,32,256]{2,1,0:T(8,128)S(1)}, u32[]{:S(2)}, u32[]{:S(2)}) collective-permute-start(f32[4,32,256]{2,1,0:T(8,128)S(1)} %get-tuple-element.58), channel_id=1, source_target_pairs={{0,2},{2,4},{4,6},{6,7},{7,5},{5,3},{3,1},{1,0},{8,10},{10,12},{12... | collective-permute-start | bytes 393224 | tf_op jit(solution)/shard_map/ppermute | solution.py:295
  332.9 3.9 collective-permute-start.19
  332.9 4.0 collective-permute-start.18
  (14 other events, 9.2 us)

commit v2 on v0

v2 whole, which is shorter than its diff:
```python
import functools

import jax
import jax.numpy as jnp
from jax import lax
from jax.experimental import pallas as pl
from jax.experimental.pallas import tpu as pltpu
from jax.sharding import PartitionSpec as P

SWEEPS = 2
VCYCLES = 2
COARSE = 8

DIFFUSE = 2.0
REACT = 0.5
OMEGA = 0.8

HALO = 4
MESH = pl.DeviceIdType.MESH


def radau_gap(count, where):
    previous = 1.0
    current = where
    for degree in range(1, count):
        following = ((2 * degree + 1) * where * current - degree * previous) / (degree + 1)
        previous = current
        current = following
    return current - previous


def radau_table(count):
    zeros_found = []
    grid_count = 4096
    lower = -1.0
    value_low = radau_gap(count, lower)
    for place in range(1, grid_count):
        upper = -1.0 + 2.0 * place / grid_count
        value_up = radau_gap(count, upper)
        if value_low * value_up < 0.0:
            left_end = lower
            right_end = upper
            left_value = value_low
            for halving in range(100):
                middle = 0.5 * (left_end + right_end)
                middle_value = radau_gap(count, middle)
                if left_value * middle_value <= 0.0:
                    right_end = middle
                else:
                    left_end = middle
                    left_value = middle_value
            zeros_found.append(0.5 * (left_end + right_end))
        lower = upper
        value_low = value_up
    zeros_found.append(1.0)
    abscissa = [(value + 1.0) / 2.0 for value in zeros_found]
    table_rows = []
    for outer in range(count):
        table_rows.append([0.0] * count)
    for column in range(count):
        factor = [1.0]
        scale = 1.0
        for other in range(count):
            if other != column:
                widened = [0.0] * (len(factor) + 1)
                for power in range(len(factor)):
                    widened[power + 1] = widened[power + 1] + factor[power]
                    widened[power] = widened[power] - abscissa[other] * factor[power]
                factor = widened
                scale = scale * (abscissa[column] - abscissa[other])
        for outer in range(count):
            upto = abscissa[outer]
            accum = 0.0
            for power in range(len(factor)):
                accum = accum + factor[power] * upto ** (power + 1) / (power + 1)
            table_rows[outer][column] = accum / scale
    return (abscissa, table_rows)


def ring_order(count):
    return list(range(0, count, 2)) + list(range(count - 1 - count % 2, 0, -2))


def rows_loop(count, body, most=4):
    step = next(k for k in range(min(most, count), 0, -1) if count % k == 0)

    def some(i, carry):
        for k in range(step):
            body(i * step + k)
        return carry

    lax.fori_loop(0, count // step, some, 0)


def pieces_of(ref):
    return [(z, x) for z in range(ref.shape[1]) for x in range(ref.shape[2])]


def six(ref, row, apart=1):
    deep, wide, tall, lanes = ref.shape[1:]
    here = {at: ref[row, at[0], at[1]] for at in pieces_of(ref)}
    totals = {}
    for z, x in here:
        total = ref[row - 1, z, x] + ref[row + 1, z, x]
        below = here[z - 1, x] if z else pltpu.roll(here[deep - 1, x], 1, 0)
        above = here[z + 1, x] if z < deep - 1 else pltpu.roll(here[0, x], tall - 1, 0)
        if wide == 1:
            left = pltpu.roll(here[z, x], apart, 1)
            right = pltpu.roll(here[z, x], lanes - apart, 1)
        else:
            left = here[z, 1 - x]
            right = pltpu.roll(left, 1 if x == 0 else lanes - 1, 1)
        totals[z, x] = total + (below + above) + (left + right)
    return here, totals


def sweep(src, src_at, source, source_at, dst, dst_at, count, shift, apart=1, most=4):
    weight = OMEGA / (1.0 + 6.0 * shift)
    spread = weight * shift

    def body(row):
        here, totals = six(src, row + src_at, apart)
        for z, x in here:
            dst[row + dst_at, z, x] = (
                (1.0 - OMEGA) * here[z, x] + weight * source[row + source_at, z, x] + spread * totals[z, x]
            )

    rows_loop(count, body, most)


def residual_sums(src, src_at, source, source_at, shift):
    first = six(src, src_at)
    second = six(src, src_at + 1)
    result = []
    for z in range(src.shape[1] // 2):
        forces, heres, sums = [], [], []
        for k, (here, totals) in enumerate((first, second)):
            for at in here:
                if at[0] // 2 == z:
                    forces.append(source[source_at + k, at[0], at[1]])
                    heres.append(here[at])
                    sums.append(totals[at])
        result.append(sum(forces) - (1.0 + 6.0 * shift) * sum(heres) + shift * sum(sums))
    return result


def copy_rows(src, src_at, dst, dst_at, count):
    def body(row):
        for z, x in pieces_of(src):
            dst[row + dst_at, z, x] = src[row + src_at, z, x]

    rows_loop(count, body, 8)


def widen(lo, mid, hi, wide):
    count = mid.shape[0]
    copy_rows(lo, 0, wide, 0, HALO)
    copy_rows(mid, 0, wide, HALO, count)
    copy_rows(hi, 0, wide, HALO + count, HALO)


def lap_and_force(wide, row, kappa):
    here, totals = six(wide, row + 1)
    for z, x in here:
        lap = totals[z, x] - 6.0 * here[z, x]
        value = here[z, x]
        force = DIFFUSE * lap + REACT * kappa[row + 1, z, x] * (value - value * value * value)
        yield (z, x), lap, force


def force_kernel(params, lo, mid, hi, first, kappa, force, base, wide):
    widen(lo, mid, hi, wide)

    def body(row):
        for (z, x), lap, value in lap_and_force(wide, row, kappa):
            force[row, z, x] = value
            base[row, z, x] = first[row + 1, z, x] - params[0] * lap

    rows_loop(force.shape[0], body)


def before(params, wide, right, field, source1, other):
    shift = params[0]
    count = wide.shape[0] - 2 * HALO
    sweep(wide, 1, right, 0, other, 0, count + 6, shift)
    sweep(other, 1, right, 1, field, 0, count + 4, shift)

    def body(row):
        for z, value in enumerate(residual_sums(field, 2 * row + 2, right, 2 * row + 3, shift)):
            source1[row, z, 0] = 0.125 * value

    rows_loop(count // 2, body, 2)


def before_first(params, wide, kappa, field, source1, right, other):
    def body(row):
        for (z, x), lap, force in lap_and_force(wide, row, kappa):
            right[row, z, x] = wide[row + 1, z, x] - params[0] * lap + params[1] * force

    rows_loop(right.shape[0], body)
    before(params, wide, right, field, source1, other)


def before_mixed(count, params, lo, mid, hi, base, *rest):
    forces, (field, source1, right, wide, other) = rest[:count], rest[count:]
    widen(lo, mid, hi, wide)

    def body(row):
        for z, x in pieces_of(base):
            total = base[row, z, x]
            for at, force in enumerate(forces):
                total = total + params[2 + at] * force[row, z, x]
            right[row, z, x] = total

    rows_loop(right.shape[0], body, 2)
    before(params, wide, right, field, source1, other)


def before_again(params, lo, mid, hi, right, field, source1, wide, other):
    widen(lo, mid, hi, wide)
    before(params, wide, right, field, source1, other)


def middle_kernel(params, lo, mid, hi, field1, wide1, source2, first):
    shift = params[0] / 4.0
    count = mid.shape[0]
    widen(lo, mid, hi, wide1)
    weight = OMEGA / (1.0 + 6.0 * shift)

    def start(row):
        for z, x in pieces_of(first):
            first[row, z, x] = weight * wide1[row, z, x]

    rows_loop(count + 2 * HALO, start, 8)
    sweep(first, 1, wide1, 1, field1, 0, count + 6, shift, 1, 11)

    def body(row):
        for z, value in enumerate(residual_sums(field1, 2 * row + 3, wide1, 2 * row + 4, shift)):
            lanes = value.shape[1]
            odd = lax.broadcasted_iota(jnp.int32, value.shape, 1) % 2 == 1
            beside = jnp.where(odd, pltpu.roll(value, 1, 1), pltpu.roll(value, lanes - 1, 1))
            source2[row, z, 0] = 0.125 * (value + beside)

    rows_loop(count // 2, body, 4)


def after_kernel(
    order, params, place, parts, field1, wide1, field, right, out, source2, even, odd, error2, more1, error1, more, last
):
    shift = params[0]
    shift1 = shift / 4.0
    shift2 = shift1 / 4.0
    devices, own = parts.shape[:2]
    rows = devices * own
    weight = OMEGA / (1.0 + 6.0 * shift2)
    for at, device in enumerate(order):
        for row in range(own):
            for z, x in pieces_of(source2):
                value = parts[device, row, z, x]
                source2[at * own + row, z, x] = value
                even[at * own + row + 1, z, x] = weight * value
    here, there = even, odd
    for step in range(COARSE - 1):
        for z, x in pieces_of(here):
            here[0, z, x] = here[rows, z, x]
            here[rows + 1, z, x] = here[1, z, x]
        sweep(here, 1, source2, 0, there, 1, rows, shift2, 2, 16)
        here, there = there, here
    begin = place[0] * own

    def pick(row):
        for z, x in pieces_of(here):
            error2[row, z, x] = here[lax.rem(begin + row - 2 + rows, rows) + 1, z, x]

    rows_loop(own + 4, pick, 12)
    count1 = 2 * own

    def correct1(row):
        for z, x in pieces_of(more1):
            more1[row, z, x] = field1[row, z, x] + error2[(row + 1) // 2, z // 2, x]

    rows_loop(count1 + 6, correct1, 11)
    sweep(more1, 1, wide1, 2, error1, 0, count1 + 4, shift1, 1, 10)
    sweep(error1, 1, wide1, 3, more1, 0, count1 + 2, shift1, 1, 9)
    count = 2 * count1

    def correct(row):
        for z, x in pieces_of(more):
            error = more1[row, z // 2, 0]
            more[2 * row, z, x] = field[2 * row, z, x] + error
            more[2 * row + 1, z, x] = field[2 * row + 1, z, x] + error

    rows_loop(count1 + 2, correct, 3)
    sweep(more, 1, right, 2, last, 0, count + 2, shift)
    sweep(last, 1, right, 3, out, 0, count, shift)


def gather_kernel(devices, part, whole, sends, takes, local):
    me = lax.axis_index("space")
    barrier = pltpu.get_barrier_semaphore()
    for turn in range(1, devices):
        pl.semaphore_signal(
            barrier, inc=1, device_id={"space": lax.rem(me + turn, devices)}, device_id_type=MESH
        )
    pl.semaphore_wait(barrier, devices - 1)
    copies = []
    for turn in range(1, devices):
        copy = pltpu.make_async_remote_copy(
            src_ref=part,
            dst_ref=whole.at[me],
            send_sem=sends.at[turn - 1],
            recv_sem=takes.at[turn - 1],
            device_id={"space": lax.rem(me + turn, devices)},
            device_id_type=MESH,
        )
        copy.start()
        copies.append(copy)
    keep = pltpu.make_async_copy(part, whole.at[me], local)
    keep.start()
    keep.wait()
    for turn, copy in enumerate(copies, 1):
        copy.wait_send()
        came = lax.rem(me - turn + devices, devices)
        pltpu.make_async_remote_copy(
            src_ref=part,
            dst_ref=whole.at[came],
            send_sem=sends.at[turn - 1],
            recv_sem=takes.at[turn - 1],
            device_id={"space": came},
            device_id_type=MESH,
        ).wait_recv()


def ring_sides(devices):
    me = lax.axis_index("space")
    half = (devices + 1) // 2
    rank = jnp.where(me % 2 == 0, me // 2, devices - 1 - me // 2)

    def device(rank):
        return jnp.where(rank < half, 2 * rank, 2 * (devices - 1 - rank) + 1)

    return device(lax.rem(rank + devices - 1, devices)), device(lax.rem(rank + 1, devices))


def halo_kernel(devices, mid, lo, hi, sends, takes):
    before_me, after_me = ring_sides(devices)
    count = mid.shape[0]
    barrier = pltpu.get_barrier_semaphore()
    for side in (before_me, after_me):
        pl.semaphore_signal(barrier, inc=1, device_id={"space": side}, device_id_type=MESH)
    pl.semaphore_wait(barrier, 2)
    copies = []
    for k, (at, dst, side) in enumerate(((count - HALO, lo, after_me), (0, hi, before_me))):
        copy = pltpu.make_async_remote_copy(
            src_ref=mid.at[pl.ds(at, HALO)],
            dst_ref=dst,
            send_sem=sends.at[k],
            recv_sem=takes.at[k],
            device_id={"space": side},
            device_id_type=MESH,
        )
        copy.start()
        copies.append(copy)
    for copy in copies:
        copy.wait()


def call(kernel, outs, scratch, *args, number=None):
    remote = number is not None
    return pl.pallas_call(
        kernel,
        out_shape=[jax.ShapeDtypeStruct(shape, jnp.float32) for shape in outs],
        in_specs=[pl.BlockSpec(memory_space=pltpu.SMEM if a.ndim == 1 else pltpu.VMEM) for a in args],
        out_specs=[pl.BlockSpec(memory_space=pltpu.VMEM)] * len(outs),
        scratch_shapes=[pltpu.VMEM(shape, jnp.float32) if isinstance(shape, tuple) else shape for shape in scratch],
        compiler_params=pltpu.CompilerParams(
            vmem_limit_bytes=60 * 2**20, collective_id=number, has_side_effects=remote
        ),
    )(*args)


def per_device(initial, kappa):
    nodes = lax.axis_size("node")
    position = lax.axis_index("node")
    devices = lax.axis_size("space")
    order = ring_order(devices)
    rank = [order.index(device) for device in range(devices)]
    place = jnp.asarray(rank, jnp.int32)[lax.axis_index("space")][None]
    across = [(i, i ^ 1) for i in range(nodes)]
    abscissa, table_rows = radau_table(nodes)
    table = jnp.asarray(table_rows, jnp.float32)
    shift = jnp.asarray([DIFFUSE * value for value in abscissa], jnp.float32)[position]

    planes, rows, cells = initial.shape
    own = rows // devices
    own1, own2 = own // 2, own // 4
    lanes = cells // 2
    shape0 = (planes, 2, devices, lanes)
    shape1 = (planes // 2, 1, devices, lanes)
    shape2 = (planes // 4, 1, devices, lanes)
    column = jnp.arange(cells)
    unweave = (column[:, None] // 2 + lanes * (column[:, None] % 2) == column[None, :]).astype(jnp.float32)

    def moved(field, matrix):
        return lax.dot_general(
            field, matrix, (((field.ndim - 1,), (0,)), ((), ())), precision=lax.Precision.HIGHEST
        )

    def halo(mid, number):
        lo, hi = call(
            functools.partial(halo_kernel, devices),
            [(HALO,) + mid.shape[1:]] * 2,
            [pltpu.SemaphoreType.DMA((2,))] * 2,
            mid, number=number,
        )
        return lo, mid, hi

    def spread_out(field):
        pieces = moved(field, unweave).reshape(planes, devices, own, cells).transpose(1, 2, 0, 3)
        pieces = jnp.stack([pieces[at] for at in rank])
        pieces = lax.all_to_all(pieces, "space", 0, 0)
        return pieces.reshape(devices, own, planes, 2, lanes).transpose(1, 2, 3, 0, 4)

    def bring_back(field):
        pieces = field.transpose(3, 0, 1, 2, 4).reshape(devices, own, planes, cells)
        pieces = lax.all_to_all(pieces, "space", 0, 0)
        pieces = jnp.stack([pieces[device] for device in order])
        return moved(pieces.transpose(2, 0, 1, 3).reshape(planes, rows, cells), unweave.T)

    first_core = position % 2 == 0
    mine = jnp.concatenate(halo(spread_out(jnp.where(first_core, initial, kappa)), 0))
    others = lax.ppermute(mine, "node", across)
    first = jnp.where(first_core, mine, others)
    strength = jnp.where(first_core, others, mine)

    extra = own + 2 * HALO
    field_outs = [(own + 4,) + shape0, (own1,) + shape1]
    right_out = [(own + 6,) + shape0]
    wide, other = (extra,) + shape0, (own + 6,) + shape0
    params = jnp.stack([shift, jnp.sum(table[position])])
    for step in range(SWEEPS):
        for cycle in range(VCYCLES):
            if cycle:
                field, source1 = call(before_again, field_outs, [wide, other], params, *parts, right)
            elif step == 0:
                field, source1, right = call(
                    before_first, field_outs + right_out, [other], params, first, strength
                )
            else:
                force, base = call(force_kernel, right_out * 2, [wide], params, *parts, first, strength)
                forces, weights = [], []
                for turn in range(nodes // 2):
                    held = force
                    if turn:
                        held = lax.ppermute(force, "node", [(i, (i + 2 * turn) % nodes) for i in range(nodes)])
                    origin = (position - 2 * turn) % nodes
                    forces += [held, lax.ppermute(held, "node", across)]
                    weights += [table[position, origin], table[position, origin ^ 1]]
                field, source1, right = call(
                    functools.partial(before_mixed, nodes),
                    field_outs + right_out, [wide, other],
                    jnp.concatenate([params, jnp.stack(weights)]), *parts, base, *forces,
                )
            field1, wide1, source2 = call(
                middle_kernel,
                [(own1 + 6,) + shape1, (own1 + 8,) + shape1, (own2,) + shape2],
                [(own1 + 8,) + shape1],
                params, *halo(source1, 1),
            )
            (whole,) = call(
                functools.partial(gather_kernel, devices),
                [(devices, own2) + shape2],
                [pltpu.SemaphoreType.DMA((devices - 1,))] * 2 + [pltpu.SemaphoreType.DMA],
                source2, number=2,
            )
            rows2 = own2 * devices
            (section,) = call(
                functools.partial(after_kernel, order),
                [(own,) + shape0],
                [
                    (rows2,) + shape2,
                    (rows2 + 2,) + shape2,
                    (rows2 + 2,) + shape2,
                    (own2 + 4,) + shape2,
                    (own1 + 6,) + shape1,
                    (own1 + 4,) + shape1,
                    (own + 4,) + shape0,
                    (own + 2,) + shape0,
                ],
                params, place, whole, field1, wide1, field, right,
            )
            if step + 1 < SWEEPS or cycle + 1 < VCYCLES:
                parts = halo(section, 0)
    return bring_back(section)[None]


def solution(mesh):
    in_specs = (P("space", None, None), P("space", None, None))
    out_specs = P("node", "space", None, None)
    return jax.shard_map(
        per_device, mesh=mesh, in_specs=in_specs, out_specs=out_specs, check_vma=False
    )
```

time: 1140 us -> 279 us (0.24)
  waiting for transfers between devices: 381 us -> 21.9 us
  local copies, waits for them, and re-layouts: 337 us -> 12.5 us
  starting transfers between devices: 252 us -> 1.57 us
  Pallas kernels: 0 us -> 173 us
  other arithmetic: 140 us -> 6.68 us
  blocking collectives: 0 us -> 58.3 us
  between operations: 19.1 us -> 0.35 us
    ppermute x132 -> x4, waiting for transfers between devices: 321 us -> 21.9 us  [the longest x1 21.9 us: per_device(): lax.ppermute(force, 'node', [(i, (i + 2 * turn) % nodes) for i in range(n...]
    reshape x4, local copies, waits for them, and re-layouts: 274 us -> 3.06 us  [the longest x2 2.12 us: spread_out(): pieces.reshape(devices, own, planes, 2, lanes).transpose(1, 2, 3, 0, 4)]
    ppermute x132 -> x4, starting transfers between devices: 252 us -> 1.57 us  [the longest x1 1.49 us: per_device(): lax.ppermute(force, 'node', [(i, (i + 2 * turn) % nodes) for i in range(n...]
    pallas_call x0 -> x25, Pallas kernels: none -> 173 us  [call(): pl.pallas_call(kernel, out_shape=[jax.ShapeDtypeStruct(shape, jnp.float32...]
    reduce_sum x14 -> x1, other arithmetic: 100 us -> 0.61 us  [per_device(): params = jnp.stack([shift, jnp.sum(table[position])])]
    all_gather x2 -> x0, waiting for transfers between devices: 59.5 us -> none  [per_device(): piece = lax.all_gather(force, 'node', axis=0, tiled=True)]
    all_to_all x0 -> x2, blocking collectives: none -> 58.3 us  [the longest x1 32.9 us: spread_out(): pieces = lax.all_to_all(pieces, 'space', 0, 0)]
    add x66 -> x1, other arithmetic: 33.1 us -> 0.01 us  [per_device(): column[:, None] // 2 + lanes * (column[:, None] % 2) == column[None, :]]
  transfers between devices with their start and end apart: 134 -> 4, of which waited for: 114 -> 1; matrix products, arithmetic and copies ran while one was open for 10% -> 3% of each run, Pallas kernels for 0% -> 0%
where the time goes in v2:
time: 279 us; the launch traced here: 278 us
  Pallas kernels  173 us (62%)
  blocking collectives  58.3 us (21%)
  waiting for transfers between devices  21.9 us (8%)
  local copies, waits for them, and re-layouts  12.5 us (4%)
  other arithmetic  6.68 us (2%)
  matrix products  3.62 us (1%)
    pallas_call x25, Pallas kernels, call(): pl.pallas_call(kernel, out_shape=[jax.ShapeDtypeStruct(shape, jnp.float32...  173 us
    all_to_all x1, blocking collectives, spread_out(): pieces = lax.all_to_all(pieces, 'space', 0, 0)  32.9 us
    all_to_all x1, blocking collectives, bring_back(): pieces = lax.all_to_all(pieces, 'space', 0, 0)  25.4 us
    ppermute x1, waiting for transfers between devices, per_device(): lax.ppermute(force, 'node', [(i, (i + 2 * turn) % nodes) for i in range(n...  21.9 us
  transfers between devices with their start and end apart: 4, of which 1 were waited for; matrix products, arithmetic and copies ran while one was open for 3% of the time, Pallas kernels for 0%

profile of v2, /device:TPU:0, one launch (start us, length us, event | category | flops | bytes accessed | tf_op | source)
XLA Modules:
  0.0 277.8 jit_solution(16261099961838539121)
XLA Ops:
  2.2 32.9 %all_to_all.10 = f32[8,32,4,256]{3,1,2,0:T(8,128)S(1)} all-to-all(f32[8,32,4,256]{3,1,2,0:T(8,128)S(1)} %slice_dynamic-update-slice_fusion.1), channel_id=1, replica_groups=mesh['node'=4,'space'=8] {'space'}, dimensions={0} | all-to-all | bytes 2097152 | tf_op jit(solution)/shard_map/all_to_all | solution.py:421
  37.2 7.0 %shard_map.55 = (f32[4,4,2,8,128]{4,3,2,1,0:T(8,128)}, f32[4,4,2,8,128]{4,3,2,1,0:T(8,128)}) custom-call(f32[32,4,2,8,128]{4,3,2,1,0:T(8,128)} %bitcast.28), custom_call_target="tpu_custom_call" | custom-call | tf_op jit(solution)/shard_map/pallas_call | solution.py:370
  52.3 8.4 %shard_map.56 = (f32[36,4,2,8,128]{4,3,2,1,0:T(8,128)}, f32[16,2,1,8,128]{4,3,2,1,0:T(8,128)}, f32[38,4,2,8,128]{4,3,2,1,0:T(8,128)}) custom-call(f32[2]{0:T(128)} %pad_maximum_fusion.1.params, f32[40,4,2,8,128]{4,3,2,1,0:T(8,128)} %get-tuple-element.86.wide.first, f32[40,4,2,8,128]{4,3,2,1,0:T(8,128)} %get-tuple-element.85.kappa), custom_call_target="tpu_custom_call" | custom-call | tf_op jit(solution)/shard_map/pallas_call | solution.py:370
  60.8 5.5 %shard_map.57 = (f32[4,2,1,8,128]{4,3,2,1,0:T(8,128)}, f32[4,2,1,8,128]{4,3,2,1,0:T(8,128)}) custom-call(f32[16,2,1,8,128]{4,3,2,1,0:T(8,128)} %get-tuple-element.47.mid), custom_call_target="tpu_custom_call" | custom-call | tf_op jit(solution)/shard_map/pallas_call | solution.py:370
  68.5 9.9 %shard_map.59.parts = f32[8,8,1,1,8,128]{5,4,3,2,1,0:T(8,128)} custom-call(f32[8,1,1,8,128]{4,3,2,1,0:T(8,128)} %get-tuple-element.50.part), custom_call_target="tpu_custom_call" | custom-call | tf_op jit(solution)/shard_map/pallas_call | solution.py:370
  78.3 9.6 %shard_map.60.mid = f32[32,4,2,8,128]{4,3,2,1,0:T(8,128)} custom-call(f32[2]{0:T(128)} %pad_maximum_fusion.1.params, s32[1]{0:T(128)} %dynamic_slice.23.place, f32[8,8,1,1,8,128]{5,4,3,2,1,0:T(8,128)} %shard_map.59.parts, f32[22,2,1,8,128]{4,3,2,1,0:T(8,128)} %get-tuple-element.51.field1, f32[24,2,1,8,128]{4,3,2,1,0:T(8,128)} %get-tuple-element.52.wide1, ...), custom_call_target="tpu_custom_call" | custom-call | tf_op jit(solution)/shard_map/pallas_call | solution.py:370
  88.0 8.0 %shard_map.61 = (f32[4,4,2,8,128]{4,3,2,1,0:T(8,128)}, f32[4,4,2,8,128]{4,3,2,1,0:T(8,128)}) custom-call(f32[32,4,2,8,128]{4,3,2,1,0:T(8,128)} %shard_map.60.mid), custom_call_target="tpu_custom_call" | custom-call | tf_op jit(solution)/shard_map/pallas_call | solution.py:370
  96.0 6.3 %shard_map.62 = (f32[36,4,2,8,128]{4,3,2,1,0:T(8,128)}, f32[16,2,1,8,128]{4,3,2,1,0:T(8,128)}) custom-call(f32[2]{0:T(128)} %pad_maximum_fusion.1.params, f32[4,4,2,8,128]{4,3,2,1,0:T(8,128)} %get-tuple-element.55.lo, f32[32,4,2,8,128]{4,3,2,1,0:T(8,128)} %shard_map.60.mid, f32[4,4,2,8,128]{4,3,2,1,0:T(8,128)} %get-tuple-element.56.hi, ...), custom_call_target="tpu_custom_call" | custom-call | tf_op jit(solution)/shard_map/pallas_call | solution.py:370
  102.3 5.7 %shard_map.63 = (f32[4,2,1,8,128]{4,3,2,1,0:T(8,128)}, f32[4,2,1,8,128]{4,3,2,1,0:T(8,128)}) custom-call(f32[16,2,1,8,128]{4,3,2,1,0:T(8,128)} %get-tuple-element.57.mid), custom_call_target="tpu_custom_call" | custom-call | tf_op jit(solution)/shard_map/pallas_call | solution.py:370
  110.2 8.3 %shard_map.65.parts = f32[8,8,1,1,8,128]{5,4,3,2,1,0:T(8,128)} custom-call(f32[8,1,1,8,128]{4,3,2,1,0:T(8,128)} %get-tuple-element.60.part), custom_call_target="tpu_custom_call" | custom-call | tf_op jit(solution)/shard_map/pallas_call | solution.py:370
  118.6 9.6 %shard_map.66.mid = f32[32,4,2,8,128]{4,3,2,1,0:T(8,128)} custom-call(f32[2]{0:T(128)} %pad_maximum_fusion.1.params, s32[1]{0:T(128)} %dynamic_slice.23.place, f32[8,8,1,1,8,128]{5,4,3,2,1,0:T(8,128)} %shard_map.65.parts, f32[22,2,1,8,128]{4,3,2,1,0:T(8,128)} %get-tuple-element.61.field1, f32[24,2,1,8,128]{4,3,2,1,0:T(8,128)} %get-tuple-element.62.wide1, ...), custom_call_target="tpu_custom_call" | custom-call | tf_op jit(solution)/shard_map/pallas_call | solution.py:370
  128.2 8.0 %shard_map.67 = (f32[4,4,2,8,128]{4,3,2,1,0:T(8,128)}, f32[4,4,2,8,128]{4,3,2,1,0:T(8,128)}) custom-call(f32[32,4,2,8,128]{4,3,2,1,0:T(8,128)} %shard_map.66.mid), custom_call_target="tpu_custom_call" | custom-call | tf_op jit(solution)/shard_map/pallas_call | solution.py:370
  136.2 5.5 %shard_map.68 = (f32[38,4,2,8,128]{4,3,2,1,0:T(8,128)}, f32[38,4,2,8,128]{4,3,2,1,0:T(8,128)}) custom-call(f32[2]{0:T(128)} %pad_maximum_fusion.1.params, f32[4,4,2,8,128]{4,3,2,1,0:T(8,128)} %get-tuple-element.64.lo, f32[32,4,2,8,128]{4,3,2,1,0:T(8,128)} %shard_map.66.mid, f32[4,4,2,8,128]{4,3,2,1,0:T(8,128)} %get-tuple-element.65.hi, ...), custom_call_target="tpu_custom_call" | custom-call | tf_op jit(solution)/shard_map/pallas_call | solution.py:370
  143.1 21.9 %collective-permute-done.2.rest_2_ = f32[38,4,2,8,128]{4,3,2,1,0:T(8,128)S(1)} collective-permute-done((f32[38,4,2,8,128]{4,3,2,1,0:T(8,128)}, f32[38,4,2,8,128]{4,3,2,1,0:T(8,128)S(1)}, u32[]{:S(2)}, u32[]{:S(2)}) %collective-permute-start.2) | collective-permute-done | bytes 1245216 | tf_op jit(solution)/shard_map/ppermute | solution.py:455
  171.1 8.7 %shard_map.69 = (f32[36,4,2,8,128]{4,3,2,1,0:T(8,128)}, f32[16,2,1,8,128]{4,3,2,1,0:T(8,128)}, f32[38,4,2,8,128]{4,3,2,1,0:T(8,128)}) custom-call(f32[6]{0:T(128)} %concatenate.7.params, f32[4,4,2,8,128]{4,3,2,1,0:T(8,128)} %get-tuple-element.64.lo, f32[32,4,2,8,128]{4,3,2,1,0:T(8,128)} %shard_map.66.mid, f32[4,4,2,8,128]{4,3,2,1,0:T(8,128)} %get-tuple-element.65.hi, ...), custom_call_target="tpu_custom_call" | custom-call | tf_op jit(solution)/shard_map/pallas_call | solution.py:370
  179.8 6.3 %shard_map.70 = (f32[4,2,1,8,128]{4,3,2,1,0:T(8,128)}, f32[4,2,1,8,128]{4,3,2,1,0:T(8,128)}) custom-call(f32[16,2,1,8,128]{4,3,2,1,0:T(8,128)} %get-tuple-element.68.mid), custom_call_target="tpu_custom_call" | custom-call | tf_op jit(solution)/shard_map/pallas_call | solution.py:370
  188.3 9.7 %shard_map.72.parts = f32[8,8,1,1,8,128]{5,4,3,2,1,0:T(8,128)} custom-call(f32[8,1,1,8,128]{4,3,2,1,0:T(8,128)} %get-tuple-element.71.part), custom_call_target="tpu_custom_call" | custom-call | tf_op jit(solution)/shard_map/pallas_call | solution.py:370
  198.0 9.6 %shard_map.73.mid = f32[32,4,2,8,128]{4,3,2,1,0:T(8,128)} custom-call(f32[2]{0:T(128)} %pad_maximum_fusion.1.params, s32[1]{0:T(128)} %dynamic_slice.23.place, f32[8,8,1,1,8,128]{5,4,3,2,1,0:T(8,128)} %shard_map.72.parts, f32[22,2,1,8,128]{4,3,2,1,0:T(8,128)} %get-tuple-element.72.field1, f32[24,2,1,8,128]{4,3,2,1,0:T(8,128)} %get-tuple-element.73.wide1, ...), custom_call_target="tpu_custom_call" | custom-call | tf_op jit(solution)/shard_map/pallas_call | solution.py:370
  207.6 7.1 %shard_map.74 = (f32[4,4,2,8,128]{4,3,2,1,0:T(8,128)}, f32[4,4,2,8,128]{4,3,2,1,0:T(8,128)}) custom-call(f32[32,4,2,8,128]{4,3,2,1,0:T(8,128)} %shard_map.73.mid), custom_call_target="tpu_custom_call" | custom-call | tf_op jit(solution)/shard_map/pallas_call | solution.py:370
  214.8 6.3 %shard_map.75 = (f32[36,4,2,8,128]{4,3,2,1,0:T(8,128)}, f32[16,2,1,8,128]{4,3,2,1,0:T(8,128)}) custom-call(f32[2]{0:T(128)} %pad_maximum_fusion.1.params, f32[4,4,2,8,128]{4,3,2,1,0:T(8,128)} %get-tuple-element.76.lo, f32[32,4,2,8,128]{4,3,2,1,0:T(8,128)} %shard_map.73.mid, f32[4,4,2,8,128]{4,3,2,1,0:T(8,128)} %get-tuple-element.77.hi, ...), custom_call_target="tpu_custom_call" | custom-call | tf_op jit(solution)/shard_map/pallas_call | solution.py:370
  221.1 6.6 %shard_map.76 = (f32[4,2,1,8,128]{4,3,2,1,0:T(8,128)}, f32[4,2,1,8,128]{4,3,2,1,0:T(8,128)}) custom-call(f32[16,2,1,8,128]{4,3,2,1,0:T(8,128)} %get-tuple-element.78.mid), custom_call_target="tpu_custom_call" | custom-call | tf_op jit(solution)/shard_map/pallas_call | solution.py:370
  229.9 8.4 %shard_map.78.parts = f32[8,8,1,1,8,128]{5,4,3,2,1,0:T(8,128)} custom-call(f32[8,1,1,8,128]{4,3,2,1,0:T(8,128)} %get-tuple-element.81.part), custom_call_target="tpu_custom_call" | custom-call | tf_op jit(solution)/shard_map/pallas_call | solution.py:370
  238.2 9.6 %shard_map.79 = f32[32,4,2,8,128]{4,3,2,1,0:T(8,128)} custom-call(f32[2]{0:T(128)} %pad_maximum_fusion.1.params, s32[1]{0:T(128)} %dynamic_slice.23.place, f32[8,8,1,1,8,128]{5,4,3,2,1,0:T(8,128)} %shard_map.78.parts, f32[22,2,1,8,128]{4,3,2,1,0:T(8,128)} %get-tuple-element.82.field1, f32[24,2,1,8,128]{4,3,2,1,0:T(8,128)} %get-tuple-element.83.wide1, ...), custom_call_target="tpu_custom_call" | custom-call | tf_op jit(solution)/shard_map/pallas_call | solution.py:370
  250.5 25.4 %all_to_all.11 = f32[8,32,4,256]{3,1,2,0:T(8,128)S(1)} all-to-all(f32[8,32,4,256]{3,1,2,0:T(8,128)S(1)} %reshape.69), channel_id=1, replica_groups=mesh['node'=4,'space'=8] {'space'}, dimensions={0} | all-to-all | bytes 2097152 | tf_op jit(solution)/shard_map/all_to_all | solution.py:426
  (58 shorter events, 33.1 us)
Async XLA Ops:
  37.2 7.0 %copy-start = (f32[8,32,4,2,128]{4,0,3,2,1:T(8,128)S(1)}, f32[8,32,4,2,128]{4,0,3,2,1:T(8,128)}, u32[]{:S(2)}) copy-start(f32[8,32,4,2,128]{4,0,3,2,1:T(8,128)} %copy.16) | copy-start | bytes 3145732
  44.3 1.3 copy-start.5
  44.3 1.9 copy-start.7
  44.3 2.5 copy-start.6
  44.3 4.9 %copy-start.3 = (f32[4,4,2,8,128]{4,3,2,1,0:T(8,128)S(1)}, f32[4,4,2,8,128]{4,3,2,1,0:T(8,128)}, u32[]{:S(2)}) copy-start(f32[4,4,2,8,128]{4,3,2,1,0:T(8,128)} %get-tuple-element.45) | copy-start | bytes 393220
  44.3 4.9 %copy-start.4 = (f32[4,4,2,8,128]{4,3,2,1,0:T(8,128)S(1)}, f32[4,4,2,8,128]{4,3,2,1,0:T(8,128)}, u32[]{:S(2)}) copy-start(f32[4,4,2,8,128]{4,3,2,1,0:T(8,128)} %get-tuple-element.46) | copy-start | bytes 393220
  45.5 3.7 %collective-permute-start = (f32[40,4,2,8,128]{4,3,2,1,0:T(8,128)S(1)}, f32[40,4,2,8,128]{4,3,2,1,0:T(8,128)}, u32[]{:S(2)}, u32[]{:S(2)}) collective-permute-start(f32[40,4,2,8,128]{4,3,2,1,0:T(8,128)S(1)} %pad_maximum_fusion), channel_id=1, source_target_pairs={{0,8},{8,0},{16,24},{24,16},{1,9},{9,1},{17,25},{25,17},{2,10},{10... | collective-permute-start | bytes 3932168 | tf_op jit(solution)/shard_map/ppermute | solution.py:432
  141.6 23.4 %collective-permute-start.2 = (f32[38,4,2,8,128]{4,3,2,1,0:T(8,128)}, f32[38,4,2,8,128]{4,3,2,1,0:T(8,128)S(1)}, u32[]{:S(2)}, u32[]{:S(2)}) collective-permute-start(f32[38,4,2,8,128]{4,3,2,1,0:T(8,128)} %get-tuple-element.67.rest_0_), channel_id=1, source_target_pairs={{0,16},{8,24},{16,0},{24,8},{1,17},{9,25},{17,1},{25,9},{2,18},{10... | collective-permute-start | bytes 3735560 | tf_op jit(solution)/shard_map/ppermute | solution.py:455
  143.1 26.9 %collective-permute-start.1 = (f32[38,4,2,8,128]{4,3,2,1,0:T(8,128)}, f32[38,4,2,8,128]{4,3,2,1,0:T(8,128)S(1)}, u32[]{:S(2)}, u32[]{:S(2)}) collective-permute-start(f32[38,4,2,8,128]{4,3,2,1,0:T(8,128)} %get-tuple-element.67.rest_0_), channel_id=1, source_target_pairs={{0,8},{8,0},{16,24},{24,16},{1,9},{9,1},{17,25},{25,17},{2,10},{10... | collective-permute-start | bytes 3735560 | tf_op jit(solution)/shard_map/ppermute | solution.py:457
  165.0 5.1 %copy-start.1 = (f32[38,4,2,8,128]{4,3,2,1,0:T(8,128)}, f32[38,4,2,8,128]{4,3,2,1,0:T(8,128)S(1)}, u32[]{:S(2)}) copy-start(f32[38,4,2,8,128]{4,3,2,1,0:T(8,128)S(1)} %collective-permute-done.2.rest_2_) | copy-start | bytes 3735556
  165.0 5.1 %collective-permute-start.3 = (f32[38,4,2,8,128]{4,3,2,1,0:T(8,128)S(1)}, f32[38,4,2,8,128]{4,3,2,1,0:T(8,128)}, u32[]{:S(2)}, u32[]{:S(2)}) collective-permute-start(f32[38,4,2,8,128]{4,3,2,1,0:T(8,128)S(1)} %collective-permute-done.2.rest_2_), channel_id=1, source_target_pairs={{0,8},{8,0},{16,24},{24,16},{1,9},{9,1},{17,25},{25,17},{2,10},{10... | collective-permute-start | bytes 3735560 | tf_op jit(solution)/shard_map/ppermute | solution.py:457
  170.1 1.1 copy-start.2

commit v3 on v2

--- a/solution.py
+++ b/solution.py
@@ -221,7 +221,11 @@
     before(params, wide, right, field, source1, other)
 
 
-def middle_kernel(params, lo, mid, hi, field1, wide1, source2, first):
+def odd_lanes(value):
+    return lax.broadcasted_iota(jnp.int32, value.shape, value.ndim - 1) % 2 == 1
+
+
+def middle(params, lo, mid, hi, field1, wide1, source2, first):
     shift = params[0] / 4.0
     count = mid.shape[0]
     widen(lo, mid, hi, wide1)
@@ -235,30 +239,37 @@
     sweep(first, 1, wide1, 1, field1, 0, count + 6, shift, 1, 11)
 
     def body(row):
-        for z, value in enumerate(residual_sums(field1, 2 * row + 3, wide1, 2 * row + 4, shift)):
-            lanes = value.shape[1]
-            odd = lax.broadcasted_iota(jnp.int32, value.shape, 1) % 2 == 1
-            beside = jnp.where(odd, pltpu.roll(value, 1, 1), pltpu.roll(value, lanes - 1, 1))
-            source2[row, z, 0] = 0.125 * (value + beside)
-
-    rows_loop(count // 2, body, 4)
-
-
-def after_kernel(
-    order, params, place, parts, field1, wide1, field, right, out, source2, even, odd, error2, more1, error1, more, last
+        evens = residual_sums(field1, 4 * row + 3, wide1, 4 * row + 4, shift)
+        odds = residual_sums(field1, 4 * row + 5, wide1, 4 * row + 6, shift)
+        for z, (low, high) in enumerate(zip(evens, odds)):
+            low = low + pltpu.roll(low, low.shape[1] - 1, 1)
+            high = high + pltpu.roll(high, 1, 1)
+            source2[row, z, 0] = 0.125 * jnp.where(odd_lanes(low), high, low)
+
+    rows_loop(count // 4, body, 2)
+
+
+def after(
+    order, params, rank, parts, field1, wide1, field, right, out, source2, even, odd, error2, more1, error1, more, last
 ):
     shift = params[0]
     shift1 = shift / 4.0
     shift2 = shift1 / 4.0
-    devices, own = parts.shape[:2]
+    devices, own = parts.shape[0], 2 * parts.shape[1]
     rows = devices * own
     weight = OMEGA / (1.0 + 6.0 * shift2)
     for at, device in enumerate(order):
-        for row in range(own):
+        for pair in range(own // 2):
             for z, x in pieces_of(source2):
-                value = parts[device, row, z, x]
-                source2[at * own + row, z, x] = value
-                even[at * own + row + 1, z, x] = weight * value
+                value = parts[device, pair, z, x]
+                odd_lane = odd_lanes(value)
+                low = jnp.where(odd_lane, pltpu.roll(value, 1, 1), value)
+                high = jnp.where(odd_lane, value, pltpu.roll(value, value.shape[1] - 1, 1))
+                row = at * own + 2 * pair
+                source2[row, z, x] = low
+                source2[row + 1, z, x] = high
+                even[row + 1, z, x] = weight * low
+                even[row + 2, z, x] = weight * high
     here, there = even, odd
     for step in range(COARSE - 1):
         for z, x in pieces_of(here):
@@ -266,7 +277,7 @@
             here[rows + 1, z, x] = here[1, z, x]
         sweep(here, 1, source2, 0, there, 1, rows, shift2, 2, 16)
         here, there = there, here
-    begin = place[0] * own
+    begin = rank * own
 
     def pick(row):
         for z, x in pieces_of(here):
@@ -295,46 +306,14 @@
     sweep(last, 1, right, 3, out, 0, count, shift)
 
 
-def gather_kernel(devices, part, whole, sends, takes, local):
+def ring_rank(devices):
     me = lax.axis_index("space")
-    barrier = pltpu.get_barrier_semaphore()
-    for turn in range(1, devices):
-        pl.semaphore_signal(
-            barrier, inc=1, device_id={"space": lax.rem(me + turn, devices)}, device_id_type=MESH
-        )
-    pl.semaphore_wait(barrier, devices - 1)
-    copies = []
-    for turn in range(1, devices):
-        copy = pltpu.make_async_remote_copy(
-            src_ref=part,
-            dst_ref=whole.at[me],
-            send_sem=sends.at[turn - 1],
-            recv_sem=takes.at[turn - 1],
-            device_id={"space": lax.rem(me + turn, devices)},
-            device_id_type=MESH,
-        )
-        copy.start()
-        copies.append(copy)
-    keep = pltpu.make_async_copy(part, whole.at[me], local)
-    keep.start()
-    keep.wait()
-    for turn, copy in enumerate(copies, 1):
-        copy.wait_send()
-        came = lax.rem(me - turn + devices, devices)
-        pltpu.make_async_remote_copy(
-            src_ref=part,
-            dst_ref=whole.at[came],
-            send_sem=sends.at[turn - 1],
-            recv_sem=takes.at[turn - 1],
-            device_id={"space": came},
-            device_id_type=MESH,
-        ).wait_recv()
+    return me // 2 + (me % 2) * (devices - 1 - 2 * (me // 2))
 
 
 def ring_sides(devices):
-    me = lax.axis_index("space")
     half = (devices + 1) // 2
-    rank = jnp.where(me % 2 == 0, me // 2, devices - 1 - me // 2)
+    rank = ring_rank(devices)
 
     def device(rank):
         return jnp.where(rank < half, 2 * rank, 2 * (devices - 1 - rank) + 1)
@@ -365,6 +344,101 @@
         copy.wait()
 
 
+def halo_copies(mid, lo, hi, sends, takes, sides):
+    before_me, after_me = sides
+    count = mid.shape[0]
+    return [
+        pltpu.make_async_remote_copy(
+            src_ref=mid.at[pl.ds(at, HALO)],
+            dst_ref=dst,
+            send_sem=sends.at[k],
+            recv_sem=takes.at[k],
+            device_id={"space": side},
+            device_id_type=MESH,
+        )
+        for k, (at, dst, side) in enumerate(((count - HALO, lo, after_me), (0, hi, before_me)))
+    ]
+
+
+def cycle_kernel(opening, inputs, order, last_cycle, params, *refs):
+    devices = len(order)
+    given, refs = refs[:inputs], refs[inputs:]
+    makes_right = opening is not before_again
+    out, *refs = refs
+    lo = hi = None
+    if not last_cycle:
+        lo, hi, *refs = refs
+    if makes_right:
+        right, *refs = refs
+    else:
+        right = given[3]
+    (
+        wide, other, field, source1, lo1, hi1, field1, wide1, packed, first1, whole,
+        source2, even, odd, error2, more1, error1, more, last,
+        sends, takes, sends1, takes1, sends2, takes2, local,
+    ) = refs
+    me = lax.axis_index("space")
+    sides = ring_sides(devices)
+    barrier = pltpu.get_barrier_semaphore()
+    for turn in range(1, devices):
+        pl.semaphore_signal(
+            barrier, inc=1, device_id={"space": lax.rem(me + turn, devices)}, device_id_type=MESH
+        )
+
+    if opening is before_first:
+        before_first(params, *given, field, source1, right, other)
+    elif opening is before_mixed:
+        before_mixed(inputs - 4, params, *given, field, source1, right, wide, other)
+    else:
+        before_again(params, *given, field, source1, wide, other)
+
+    pl.semaphore_wait(barrier, devices - 1)
+    copies = halo_copies(source1, lo1, hi1, sends1, takes1, sides)
+    for copy in copies:
+        copy.start()
+    for copy in copies:
+        copy.wait()
+    middle(params, lo1, source1, hi1, field1, wide1, packed, first1)
+
+    copies = []
+    for turn in range(1, devices):
+        copy = pltpu.make_async_remote_copy(
+            src_ref=packed,
+            dst_ref=whole.at[me],
+            send_sem=sends2.at[turn - 1],
+            recv_sem=takes2.at[turn - 1],
+            device_id={"space": lax.rem(me + turn, devices)},
+            device_id_type=MESH,
+        )
+        copy.start()
+        copies.append(copy)
+    keep = pltpu.make_async_copy(packed, whole.at[me], local)
+    keep.start()
+    keep.wait()
+    for turn, copy in enumerate(copies, 1):
+        copy.wait_send()
+        came = lax.rem(me - turn + devices, devices)
+        pltpu.make_async_remote_copy(
+            src_ref=packed,
+            dst_ref=whole.at[came],
+            send_sem=sends2.at[turn - 1],
+            recv_sem=takes2.at[turn - 1],
+            device_id={"space": came},
+            device_id_type=MESH,
+        ).wait_recv()
+
+    after(
+        order, params, ring_rank(devices), whole, field1, wide1, field, right, out,
+        source2, even, odd, error2, more1, error1, more, last,
+    )
+    if not last_cycle:
+        copies = halo_copies(out, lo, hi, sends, takes, sides)
+        for copy in copies:
+            copy.start()
+        for copy in copies:
+            copy.wait()
+
+
 def call(kernel, outs, scratch, *args, number=None):
     remote = number is not None
     return pl.pallas_call(
@@ -434,20 +508,42 @@
     strength = jnp.where(first_core, others, mine)
 
     extra = own + 2 * HALO
-    field_outs = [(own + 4,) + shape0, (own1,) + shape1]
+    rows2 = own2 * devices
     right_out = [(own + 6,) + shape0]
-    wide, other = (extra,) + shape0, (own + 6,) + shape0
+    edges = [(HALO,) + shape0] * 2
+    dma = pltpu.SemaphoreType.DMA
+    scratch = [
+        (extra,) + shape0,
+        (own + 6,) + shape0,
+        (own + 4,) + shape0,
+        (own1,) + shape1,
+        (HALO,) + shape1,
+        (HALO,) + shape1,
+        (own1 + 6,) + shape1,
+        (own1 + 8,) + shape1,
+        (own2 // 2,) + shape2,
+        (own1 + 8,) + shape1,
+        (devices, own2 // 2) + shape2,
+        (rows2,) + shape2,
+        (rows2 + 2,) + shape2,
+        (rows2 + 2,) + shape2,
+        (own2 + 4,) + shape2,
+        (own1 + 6,) + shape1,
+        (own1 + 4,) + shape1,
+        (own + 4,) + shape0,
+        (own + 2,) + shape0,
+        dma((2,)), dma((2,)), dma((2,)), dma((2,)), dma((devices - 1,)), dma((devices - 1,)), dma,
+    ]
     params = jnp.stack([shift, jnp.sum(table[position])])
     for step in range(SWEEPS):
         for cycle in range(VCYCLES):
+            scalars = params
             if cycle:
-                field, source1 = call(before_again, field_outs, [wide, other], params, *parts, right)
+                opening, given = before_again, (*parts, right)
             elif step == 0:
-                field, source1, right = call(
-                    before_first, field_outs + right_out, [other], params, first, strength
-                )
+                opening, given = before_first, (first, strength)
             else:
-                force, base = call(force_kernel, right_out * 2, [wide], params, *parts, first, strength)
+                force, base = call(force_kernel, right_out * 2, [scratch[0]], params, *parts, first, strength)
                 forces, weights = [], []
                 for turn in range(nodes // 2):
                     held = force
@@ -456,41 +552,19 @@
                     origin = (position - 2 * turn) % nodes
                     forces += [held, lax.ppermute(held, "node", across)]
                     weights += [table[position, origin], table[position, origin ^ 1]]
-                field, source1, right = call(
-                    functools.partial(before_mixed, nodes),
-                    field_outs + right_out, [wide, other],
-                    jnp.concatenate([params, jnp.stack(weights)]), *parts, base, *forces,
-                )
-            field1, wide1, source2 = call(
-                middle_kernel,
-                [(own1 + 6,) + shape1, (own1 + 8,) + shape1, (own2,) + shape2],
-                [(own1 + 8,) + shape1],
-                params, *halo(source1, 1),
+                scalars = jnp.concatenate([params, jnp.stack(weights)])
+                opening, given = before_mixed, (*parts, base, *forces)
+            last_cycle = step + 1 == SWEEPS and cycle + 1 == VCYCLES
+            section, *rest = call(
+                functools.partial(cycle_kernel, opening, len(given), order, last_cycle),
+                [(own,) + shape0] + ([] if last_cycle else edges) + ([] if cycle else right_out),
+                scratch,
+                scalars, *given, number=1 + 2 * step + cycle,
             )
-            (whole,) = call(
-                functools.partial(gather_kernel, devices),
-                [(devices, own2) + shape2],
-                [pltpu.SemaphoreType.DMA((devices - 1,))] * 2 + [pltpu.SemaphoreType.DMA],
-                source2, number=2,
-            )
-            rows2 = own2 * devices
-            (section,) = call(
-                functools.partial(after_kernel, order),
-                [(own,) + shape0],
-                [
-                    (rows2,) + shape2,
-                    (rows2 + 2,) + shape2,
-                    (rows2 + 2,) + shape2,
-                    (own2 + 4,) + shape2,
-                    (own1 + 6,) + shape1,
-                    (own1 + 4,) + shape1,
-                    (own + 4,) + shape0,
-                    (own + 2,) + shape0,
-                ],
-                params, place, whole, field1, wide1, field, right,
-            )
-            if step + 1 < SWEEPS or cycle + 1 < VCYCLES:
-                parts = halo(section, 0)
+            if not last_cycle:
+                parts = (rest[0], section, rest[1])
+            if not cycle:
+                right = rest[-1]
     return bring_back(section)[None]
 
 

time: 279 us -> 226 us (0.81)
  Pallas kernels: 173 us -> 116 us
  waiting for transfers between devices: 21.9 us -> 24.8 us
    pallas_call x25 -> x6, Pallas kernels: 173 us -> 116 us  [call(): pl.pallas_call(kernel, out_shape=[jax.ShapeDtypeStruct(shape, jnp.float32...]
    ppermute x1, waiting for transfers between devices: 21.9 us -> 24.8 us  [per_device(): lax.ppermute(force, 'node', [(i, (i + 2 * turn) % nodes) for i in range(n...]
  transfers between devices with their start and end apart: 4 -> 4, of which waited for: 1 -> 1; matrix products, arithmetic and copies ran while one was open for 3% -> 4% of each run, Pallas kernels for 0% -> 0%
where the time goes in v3:
time: 226 us; the launch traced here: 225 us
  Pallas kernels  116 us (51%)
  blocking collectives  59.9 us (27%)
  waiting for transfers between devices  24.8 us (11%)
  local copies, waits for them, and re-layouts  11.9 us (5%)
  other arithmetic  6.85 us (3%)
  matrix products  3.62 us (2%)
    pallas_call x6, Pallas kernels, call(): pl.pallas_call(kernel, out_shape=[jax.ShapeDtypeStruct(shape, jnp.float32...  116 us
    all_to_all x1, blocking collectives, spread_out(): pieces = lax.all_to_all(pieces, 'space', 0, 0)  32.9 us
    all_to_all x1, blocking collectives, bring_back(): pieces = lax.all_to_all(pieces, 'space', 0, 0)  27 us
    ppermute x1, waiting for transfers between devices, per_device(): lax.ppermute(force, 'node', [(i, (i + 2 * turn) % nodes) for i in range(n...  24.8 us
  transfers between devices with their start and end apart: 4, of which 1 were waited for; matrix products, arithmetic and copies ran while one was open for 4% of the time, Pallas kernels for 0%

profile of v3, /device:TPU:0, one launch (start us, length us, event | category | flops | bytes accessed | tf_op | source)
XLA Modules:
  0.0 225.3 jit_solution(4525326914585850168)
XLA Ops:
  0.0 1.9 fusion
  2.2 32.9 %all_to_all.10 = f32[8,32,4,256]{3,1,2,0:T(8,128)S(1)} all-to-all(f32[8,32,4,256]{3,1,2,0:T(8,128)S(1)} %slice_dynamic-update-slice_fusion.1), channel_id=1, replica_groups=mesh['node'=4,'space'=8] {'space'}, dimensions={0} | all-to-all | bytes 2097152 | tf_op jit(solution)/shard_map/all_to_all | solution.py:495
  35.1 0.5 reshape.68
  35.6 1.6 copy.15
  37.2 7.0 %shard_map.46 = (f32[4,4,2,8,128]{4,3,2,1,0:T(8,128)}, f32[4,4,2,8,128]{4,3,2,1,0:T(8,128)}) custom-call(f32[32,4,2,8,128]{4,3,2,1,0:T(8,128)} %bitcast.28), custom_call_target="tpu_custom_call" | custom-call | tf_op jit(solution)/shard_map/pallas_call | solution.py:444
  44.3 1.1 pad_maximum_fusion
  45.5 0.6 dynamic-slice_reduce_fusion
  46.1 0.6 dynamic_slice.18
  46.8 1.9 pad_maximum_fusion.1.params
  48.7 3.1 %broadcast_select_fusion = (f32[40,4,2,8,128]{4,3,2,1,0:T(8,128)}, f32[40,4,2,8,128]{4,3,2,1,0:T(8,128)}) fusion(f32[40,4,2,8,128]{4,3,2,1,0:T(8,128)} %collective-permute-done, pred[]{:T(512)S(6)} %eq.28, f32[4,4,2,8,128]{4,3,2,1,0:T(8,128)S(1)} %copy-done.4, f32[32,4,2,8,128]{4,3,2,1,0:T(8,128)S(1)} %bitcast.30, f32[4,4,2,8,128]{4,3,2,1,0:T(8,128)S(1)} %copy-done.3), kind=kLoop, calls=%fused_computation.6 | loop fusion | flops 1310720 | bytes 5242881 | tf_op jit(solution)/shard_map/jit(_where)/select_n | solution.py:508
  51.9 28.7 %shard_map.47 = (f32[32,4,2,8,128]{4,3,2,1,0:T(8,128)}, f32[4,4,2,8,128]{4,3,2,1,0:T(8,128)}, f32[4,4,2,8,128]{4,3,2,1,0:T(8,128)}, f32[38,4,2,8,128]{4,3,2,1,0:T(8,128)}) custom-call(f32[2]{0:T(128)} %pad_maximum_fusion.1.params, f32[40,4,2,8,128]{4,3,2,1,0:T(8,128)} %get-tuple-element.36.refs_0_.first, f32[40,4,2,8,128]{4,3,2,1,0:T(8,128)} %get-tuple-element.35.refs_1_.kappa), custom_call_target="tpu_custom_call" | custom-call | tf_op jit(solution)/shard_map/pallas_call | solution.py:444
  80.6 24.8 %shard_map.48 = (f32[32,4,2,8,128]{4,3,2,1,0:T(8,128)}, f32[4,4,2,8,128]{4,3,2,1,0:T(8,128)}, f32[4,4,2,8,128]{4,3,2,1,0:T(8,128)}) custom-call(f32[2]{0:T(128)} %pad_maximum_fusion.1.params, f32[4,4,2,8,128]{4,3,2,1,0:T(8,128)} %get-tuple-element.22.refs_0_, f32[32,4,2,8,128]{4,3,2,1,0:T(8,128)} %get-tuple-element.23.refs_1_, ...), custom_call_target="tpu_custom_call" | custom-call | tf_op jit(solution)/shard_map/pallas_call | solution.py:444
  105.4 5.4 %shard_map.49 = (f32[38,4,2,8,128]{4,3,2,1,0:T(8,128)}, f32[38,4,2,8,128]{4,3,2,1,0:T(8,128)}) custom-call(f32[2]{0:T(128)} %pad_maximum_fusion.1.params, f32[4,4,2,8,128]{4,3,2,1,0:T(8,128)} %get-tuple-element.26.lo.refs_0_, f32[32,4,2,8,128]{4,3,2,1,0:T(8,128)} %get-tuple-element.27.mid.refs_1_, f32[4,4,2,8,128]{4,3,2,1,0:T(8,128)} %get-tuple-element.28.hi.refs_2_, ...), custom_call_target="tpu_custom_call" | custom-call | tf_op jit(solution)/shard_map/pallas_call | solution.py:444
  110.9 1.5 collective-permute-start.2
  112.4 24.8 %collective-permute-done.2.refs_6_ = f32[38,4,2,8,128]{4,3,2,1,0:T(8,128)S(1)} collective-permute-done((f32[38,4,2,8,128]{4,3,2,1,0:T(8,128)}, f32[38,4,2,8,128]{4,3,2,1,0:T(8,128)S(1)}, u32[]{:S(2)}, u32[]{:S(2)}) %collective-permute-start.2) | collective-permute-done | bytes 1245216 | tf_op jit(solution)/shard_map/ppermute | solution.py:551
  137.2 0.8 fusion.12
  137.9 4.4 %concatenate.7.params = f32[6]{0:T(128)} concatenate(f32[1]{0:T(128)} %dynamic_slice.18, f32[1]{0:T(128)} %bitcast, f32[1]{0:T(128)} %bitcast.1, f32[1]{0:T(128)} %bitcast.2, f32[1]{0:T(128)} %bitcast.3, f32[1]{0:T(128)} %bitcast.4), dimensions={0} | concatenate | bytes 48 | tf_op jit(solution)/shard_map/concatenate | solution.py:555
  142.3 1.0 copy-done.2
  143.3 29.2 %shard_map.50 = (f32[32,4,2,8,128]{4,3,2,1,0:T(8,128)}, f32[4,4,2,8,128]{4,3,2,1,0:T(8,128)}, f32[4,4,2,8,128]{4,3,2,1,0:T(8,128)}, f32[38,4,2,8,128]{4,3,2,1,0:T(8,128)}) custom-call(f32[6]{0:T(128)} %concatenate.7.params, f32[4,4,2,8,128]{4,3,2,1,0:T(8,128)} %get-tuple-element.26.lo.refs_0_, f32[32,4,2,8,128]{4,3,2,1,0:T(8,128)} %get-tuple-element.27.mid.refs_1_, ...), custom_call_target="tpu_custom_call" | custom-call | tf_op jit(solution)/shard_map/pallas_call | solution.py:444
  172.5 21.2 %shard_map.51 = f32[32,4,2,8,128]{4,3,2,1,0:T(8,128)} custom-call(f32[2]{0:T(128)} %pad_maximum_fusion.1.params, f32[4,4,2,8,128]{4,3,2,1,0:T(8,128)} %get-tuple-element.31.refs_0_, f32[32,4,2,8,128]{4,3,2,1,0:T(8,128)} %get-tuple-element.32.refs_1_, f32[4,4,2,8,128]{4,3,2,1,0:T(8,128)} %get-tuple-element.33.refs_2_, ...), custom_call_target="tpu_custom_call" | custom-call | tf_op jit(solution)/shard_map/pallas_call | solution.py:444
  193.7 1.8 copy.11
  195.5 0.8 reshape.69
  196.4 27.0 %all_to_all.11 = f32[8,32,4,256]{3,1,2,0:T(8,128)S(1)} all-to-all(f32[8,32,4,256]{3,1,2,0:T(8,128)S(1)} %reshape.69), channel_id=1, replica_groups=mesh['node'=4,'space'=8] {'space'}, dimensions={0} | all-to-all | bytes 2097152 | tf_op jit(solution)/shard_map/all_to_all | solution.py:500
  223.7 1.7 convolution_bitcast_fusion
  (36 shorter events, 0.5 us)
Async XLA Ops:
  37.2 7.0 %copy-start = (f32[8,32,4,2,128]{4,0,3,2,1:T(8,128)S(1)}, f32[8,32,4,2,128]{4,0,3,2,1:T(8,128)}, u32[]{:S(2)}) copy-start(f32[8,32,4,2,128]{4,0,3,2,1:T(8,128)} %copy.15) | copy-start | bytes 3145732
  44.2 1.3 copy-start.5
  44.3 1.9 copy-start.6
  44.3 4.5 %copy-start.3 = (f32[4,4,2,8,128]{4,3,2,1,0:T(8,128)S(1)}, f32[4,4,2,8,128]{4,3,2,1,0:T(8,128)}, u32[]{:S(2)}) copy-start(f32[4,4,2,8,128]{4,3,2,1,0:T(8,128)} %get-tuple-element.20) | copy-start | bytes 393220
  44.3 4.5 %copy-start.4 = (f32[4,4,2,8,128]{4,3,2,1,0:T(8,128)S(1)}, f32[4,4,2,8,128]{4,3,2,1,0:T(8,128)}, u32[]{:S(2)}) copy-start(f32[4,4,2,8,128]{4,3,2,1,0:T(8,128)} %get-tuple-element.21) | copy-start | bytes 393220
  45.4 3.3 %collective-permute-start = (f32[40,4,2,8,128]{4,3,2,1,0:T(8,128)S(1)}, f32[40,4,2,8,128]{4,3,2,1,0:T(8,128)}, u32[]{:S(2)}, u32[]{:S(2)}) collective-permute-start(f32[40,4,2,8,128]{4,3,2,1,0:T(8,128)S(1)} %pad_maximum_fusion), channel_id=1, source_target_pairs={{0,8},{8,0},{16,24},{24,16},{1,9},{9,1},{17,25},{25,17},{2,10},{10... | collective-permute-start | bytes 3932168 | tf_op jit(solution)/shard_map/ppermute | solution.py:506
  110.9 26.3 %collective-permute-start.2 = (f32[38,4,2,8,128]{4,3,2,1,0:T(8,128)}, f32[38,4,2,8,128]{4,3,2,1,0:T(8,128)S(1)}, u32[]{:S(2)}, u32[]{:S(2)}) collective-permute-start(f32[38,4,2,8,128]{4,3,2,1,0:T(8,128)} %get-tuple-element.30.refs_4_), channel_id=1, source_target_pairs={{0,16},{8,24},{16,0},{24,8},{1,17},{9,25},{17,1},{25,9},{2,18},{10... | collective-permute-start | bytes 3735560 | tf_op jit(solution)/shard_map/ppermute | solution.py:551
  112.4 29.9 %collective-permute-start.1 = (f32[38,4,2,8,128]{4,3,2,1,0:T(8,128)}, f32[38,4,2,8,128]{4,3,2,1,0:T(8,128)S(1)}, u32[]{:S(2)}, u32[]{:S(2)}) collective-permute-start(f32[38,4,2,8,128]{4,3,2,1,0:T(8,128)} %get-tuple-element.30.refs_4_), channel_id=1, source_target_pairs={{0,8},{8,0},{16,24},{24,16},{1,9},{9,1},{17,25},{25,17},{2,10},{10... | collective-permute-start | bytes 3735560 | tf_op jit(solution)/shard_map/ppermute | solution.py:553
  137.2 5.2 %copy-start.1 = (f32[38,4,2,8,128]{4,3,2,1,0:T(8,128)}, f32[38,4,2,8,128]{4,3,2,1,0:T(8,128)S(1)}, u32[]{:S(2)}) copy-start(f32[38,4,2,8,128]{4,3,2,1,0:T(8,128)S(1)} %collective-permute-done.2.refs_6_) | copy-start | bytes 3735556
  137.2 5.2 %collective-permute-start.3 = (f32[38,4,2,8,128]{4,3,2,1,0:T(8,128)S(1)}, f32[38,4,2,8,128]{4,3,2,1,0:T(8,128)}, u32[]{:S(2)}, u32[]{:S(2)}) collective-permute-start(f32[38,4,2,8,128]{4,3,2,1,0:T(8,128)S(1)} %collective-permute-done.2.refs_6_), channel_id=1, source_target_pairs={{0,8},{8,0},{16,24},{24,16},{1,9},{9,1},{17,25},{25,17},{2,10},{10... | collective-permute-start | bytes 3735560 | tf_op jit(solution)/shard_map/ppermute | solution.py:553
  142.3 1.0 copy-start.2

commit v4 on v3

--- a/solution.py
+++ b/solution.py
@@ -459,11 +459,14 @@
     devices = lax.axis_size("space")
     order = ring_order(devices)
     rank = [order.index(device) for device in range(devices)]
-    place = jnp.asarray(rank, jnp.int32)[lax.axis_index("space")][None]
     across = [(i, i ^ 1) for i in range(nodes)]
     abscissa, table_rows = radau_table(nodes)
-    table = jnp.asarray(table_rows, jnp.float32)
-    shift = jnp.asarray([DIFFUSE * value for value in abscissa], jnp.float32)[position]
+    scalars = []
+    for node in range(nodes):
+        weights = table_rows[node]
+        turned = [weights[((node - 2 * turn) % nodes) ^ side] for turn in range(nodes // 2) for side in range(2)]
+        scalars.append([DIFFUSE * abscissa[node], sum(weights)] + turned)
+    params = lax.dynamic_index_in_dim(jnp.asarray(scalars, jnp.float32), position, 0, False)
 
     planes, rows, cells = initial.shape
     own = rows // devices
@@ -534,32 +537,27 @@
         (own + 2,) + shape0,
         dma((2,)), dma((2,)), dma((2,)), dma((2,)), dma((devices - 1,)), dma((devices - 1,)), dma,
     ]
-    params = jnp.stack([shift, jnp.sum(table[position])])
     for step in range(SWEEPS):
         for cycle in range(VCYCLES):
-            scalars = params
             if cycle:
                 opening, given = before_again, (*parts, right)
             elif step == 0:
                 opening, given = before_first, (first, strength)
             else:
                 force, base = call(force_kernel, right_out * 2, [scratch[0]], params, *parts, first, strength)
-                forces, weights = [], []
+                forces = []
                 for turn in range(nodes // 2):
                     held = force
                     if turn:
                         held = lax.ppermute(force, "node", [(i, (i + 2 * turn) % nodes) for i in range(nodes)])
-                    origin = (position - 2 * turn) % nodes
                     forces += [held, lax.ppermute(held, "node", across)]
-                    weights += [table[position, origin], table[position, origin ^ 1]]
-                scalars = jnp.concatenate([params, jnp.stack(weights)])
                 opening, given = before_mixed, (*parts, base, *forces)
             last_cycle = step + 1 == SWEEPS and cycle + 1 == VCYCLES
             section, *rest = call(
                 functools.partial(cycle_kernel, opening, len(given), order, last_cycle),
                 [(own,) + shape0] + ([] if last_cycle else edges) + ([] if cycle else right_out),
                 scratch,
-                scalars, *given, number=1 + 2 * step + cycle,
+                params, *given, number=1 + 2 * step + cycle,
             )
             if not last_cycle:
                 parts = (rest[0], section, rest[1])

time: 226 us -> 219 us (0.969)
  local copies, waits for them, and re-layouts: 11.9 us -> 7.36 us
  waiting for transfers between devices: 24.8 us -> 28 us
  other arithmetic: 6.85 us -> 4.29 us
    concatenate x1 -> x0, local copies, waits for them, and re-layouts: 4.37 us -> none  [per_device(): scalars = jnp.concatenate([params, jnp.stack(weights)])]
    ppermute x2, waiting for transfers between devices: 0.01 us -> 2.93 us  [per_device(): forces += [held, lax.ppermute(held, 'node', across)]]
  transfers between devices with their start and end apart: 4 -> 4, of which waited for: 1 -> 3; matrix products, arithmetic and copies ran while one was open for 4% -> 1% of each run, Pallas kernels for 0% -> 0%
where the time goes in v4:
time: 219 us; the launch traced here: 218 us
  Pallas kernels  114 us (52%)
  blocking collectives  58.5 us (27%)
  waiting for transfers between devices  28 us (13%)
  local copies, waits for them, and re-layouts  7.36 us (3%)
  other arithmetic  4.29 us (2%)
  matrix products  3.62 us (2%)
    pallas_call x6, Pallas kernels, call(): pl.pallas_call(kernel, out_shape=[jax.ShapeDtypeStruct(shape, jnp.float32...  114 us
    all_to_all x1, blocking collectives, spread_out(): pieces = lax.all_to_all(pieces, 'space', 0, 0)  32.9 us
    all_to_all x1, blocking collectives, bring_back(): pieces = lax.all_to_all(pieces, 'space', 0, 0)  25.7 us
    ppermute x1, waiting for transfers between devices, per_device(): lax.ppermute(force, 'node', [(i, (i + 2 * turn) % nodes) for i in range(n...  23.1 us
  transfers between devices with their start and end apart: 4, of which 3 were waited for; matrix products, arithmetic and copies ran while one was open for 1% of the time, Pallas kernels for 0%

profile of v4, /device:TPU:0, one launch (start us, length us, event | category | flops | bytes accessed | tf_op | source)
XLA Modules:
  0.0 218.1 jit_solution(8475874955345262696)
XLA Ops:
  0.0 1.9 fusion
  2.0 0.1 copy.11
  2.2 32.9 %all_to_all.10 = f32[8,32,4,256]{3,1,2,0:T(8,128)S(1)} all-to-all(f32[8,32,4,256]{3,1,2,0:T(8,128)S(1)} %slice_dynamic-update-slice_fusion.1), channel_id=1, replica_groups=mesh['node'=4,'space'=8] {'space'}, dimensions={0} | all-to-all | bytes 2097152 | tf_op jit(solution)/shard_map/all_to_all | solution.py:498
  35.1 0.5 reshape.68
  35.6 1.6 copy.10
  37.2 7.0 %shard_map.37 = (f32[4,4,2,8,128]{4,3,2,1,0:T(8,128)}, f32[4,4,2,8,128]{4,3,2,1,0:T(8,128)}) custom-call(f32[32,4,2,8,128]{4,3,2,1,0:T(8,128)} %bitcast.25), custom_call_target="tpu_custom_call" | custom-call | tf_op jit(solution)/shard_map/pallas_call | solution.py:444
  44.3 1.1 pad_maximum_fusion
  45.5 1.2 dynamic-slice_bitcast_fusion.params
  46.7 1.9 collective-permute-done
  48.7 3.1 %broadcast_select_fusion = (f32[40,4,2,8,128]{4,3,2,1,0:T(8,128)}, f32[40,4,2,8,128]{4,3,2,1,0:T(8,128)}) fusion(f32[40,4,2,8,128]{4,3,2,1,0:T(8,128)} %collective-permute-done, pred[]{:T(512)S(6)} %eq.26, f32[4,4,2,8,128]{4,3,2,1,0:T(8,128)S(1)} %copy-done.5, f32[32,4,2,8,128]{4,3,2,1,0:T(8,128)S(1)} %bitcast.27, f32[4,4,2,8,128]{4,3,2,1,0:T(8,128)S(1)} %copy-done.4), kind=kLoop, calls=%fused_computation.6 | loop fusion | flops 1310720 | bytes 5242881 | tf_op jit(solution)/shard_map/jit(_where)/select_n | solution.py:511
  51.8 27.6 %shard_map.38 = (f32[32,4,2,8,128]{4,3,2,1,0:T(8,128)}, f32[4,4,2,8,128]{4,3,2,1,0:T(8,128)}, f32[4,4,2,8,128]{4,3,2,1,0:T(8,128)}, f32[38,4,2,8,128]{4,3,2,1,0:T(8,128)}) custom-call(f32[6]{0:T(128)} %dynamic-slice_bitcast_fusion.params, f32[40,4,2,8,128]{4,3,2,1,0:T(8,128)} %get-tuple-element.36.refs_0_.first, ...), custom_call_target="tpu_custom_call" | custom-call | tf_op jit(solution)/shard_map/pallas_call | solution.py:444
  79.4 25.9 %shard_map.39 = (f32[32,4,2,8,128]{4,3,2,1,0:T(8,128)}, f32[4,4,2,8,128]{4,3,2,1,0:T(8,128)}, f32[4,4,2,8,128]{4,3,2,1,0:T(8,128)}) custom-call(f32[6]{0:T(128)} %dynamic-slice_bitcast_fusion.params, f32[4,4,2,8,128]{4,3,2,1,0:T(8,128)} %get-tuple-element.22.refs_0_, f32[32,4,2,8,128]{4,3,2,1,0:T(8,128)} %get-tuple-element.23.refs_1_, ...), custom_call_target="tpu_custom_call" | custom-call | tf_op jit(solution)/shard_map/pallas_call | solution.py:444
  105.3 5.4 %shard_map.40 = (f32[38,4,2,8,128]{4,3,2,1,0:T(8,128)}, f32[38,4,2,8,128]{4,3,2,1,0:T(8,128)}) custom-call(f32[6]{0:T(128)} %dynamic-slice_bitcast_fusion.params, f32[4,4,2,8,128]{4,3,2,1,0:T(8,128)} %get-tuple-element.26.lo.refs_0_, f32[32,4,2,8,128]{4,3,2,1,0:T(8,128)} %get-tuple-element.27.mid.refs_1_, f32[4,4,2,8,128]{4,3,2,1,0:T(8,128)} %get-tuple-element.28.hi.refs_2_, ...), custom_call_target="tpu_custom_call" | custom-call | tf_op jit(solution)/shard_map/pallas_call | solution.py:444
  110.8 1.5 collective-permute-start.2
  112.3 23.1 %collective-permute-done.2.refs_6_ = f32[38,4,2,8,128]{4,3,2,1,0:T(8,128)S(1)} collective-permute-done((f32[38,4,2,8,128]{4,3,2,1,0:T(8,128)}, f32[38,4,2,8,128]{4,3,2,1,0:T(8,128)S(1)}, u32[]{:S(2)}, u32[]{:S(2)}) %collective-permute-start.2) | collective-permute-done | bytes 1245216 | tf_op jit(solution)/shard_map/ppermute | solution.py:552
  135.4 2.9 %collective-permute-done.3.refs_7_ = f32[38,4,2,8,128]{4,3,2,1,0:T(8,128)S(1)} collective-permute-done((f32[38,4,2,8,128]{4,3,2,1,0:T(8,128)S(1)}, f32[38,4,2,8,128]{4,3,2,1,0:T(8,128)S(1)}, u32[]{:S(2)}, u32[]{:S(2)}) %collective-permute-start.3) | collective-permute-done | bytes 1245216 | tf_op jit(solution)/shard_map/ppermute | solution.py:553
  138.3 1.0 copy-done.3
  139.4 27.1 %shard_map.41 = (f32[32,4,2,8,128]{4,3,2,1,0:T(8,128)}, f32[4,4,2,8,128]{4,3,2,1,0:T(8,128)}, f32[4,4,2,8,128]{4,3,2,1,0:T(8,128)}, f32[38,4,2,8,128]{4,3,2,1,0:T(8,128)}) custom-call(f32[6]{0:T(128)} %dynamic-slice_bitcast_fusion.params, f32[4,4,2,8,128]{4,3,2,1,0:T(8,128)} %get-tuple-element.26.lo.refs_0_, ...), custom_call_target="tpu_custom_call" | custom-call | tf_op jit(solution)/shard_map/pallas_call | solution.py:444
  166.4 21.4 %shard_map.42 = f32[32,4,2,8,128]{4,3,2,1,0:T(8,128)} custom-call(f32[6]{0:T(128)} %dynamic-slice_bitcast_fusion.params, f32[4,4,2,8,128]{4,3,2,1,0:T(8,128)} %get-tuple-element.31.refs_0_, f32[32,4,2,8,128]{4,3,2,1,0:T(8,128)} %get-tuple-element.32.refs_1_, f32[4,4,2,8,128]{4,3,2,1,0:T(8,128)} %get-tuple-element.33.refs_2_, ...), custom_call_target="tpu_custom_call" | custom-call | tf_op jit(solution)/shard_map/pallas_call | solution.py:444
  187.9 1.8 copy.6
  189.7 0.8 reshape.69
  190.5 25.7 %all_to_all.11 = f32[8,32,4,256]{3,1,2,0:T(8,128)S(1)} all-to-all(f32[8,32,4,256]{3,1,2,0:T(8,128)S(1)} %reshape.69), channel_id=1, replica_groups=mesh['node'=4,'space'=8] {'space'}, dimensions={0} | all-to-all | bytes 2097152 | tf_op jit(solution)/shard_map/all_to_all | solution.py:503
  216.3 0.1 copy.7
  216.4 1.7 convolution_bitcast_fusion
  (30 shorter events, 0.3 us)
Async XLA Ops:
  37.2 7.0 %copy-start = (f32[8,32,4,2,128]{4,0,3,2,1:T(8,128)S(1)}, f32[8,32,4,2,128]{4,0,3,2,1:T(8,128)}, u32[]{:S(2)}) copy-start(f32[8,32,4,2,128]{4,0,3,2,1:T(8,128)} %copy.10) | copy-start | bytes 3145732
  44.2 4.4 %copy-start.4 = (f32[4,4,2,8,128]{4,3,2,1,0:T(8,128)S(1)}, f32[4,4,2,8,128]{4,3,2,1,0:T(8,128)}, u32[]{:S(2)}) copy-start(f32[4,4,2,8,128]{4,3,2,1,0:T(8,128)} %get-tuple-element.20) | copy-start | bytes 393220
  44.3 4.4 %copy-start.5 = (f32[4,4,2,8,128]{4,3,2,1,0:T(8,128)S(1)}, f32[4,4,2,8,128]{4,3,2,1,0:T(8,128)}, u32[]{:S(2)}) copy-start(f32[4,4,2,8,128]{4,3,2,1,0:T(8,128)} %get-tuple-element.21) | copy-start | bytes 393220
  45.4 3.2 %collective-permute-start = (f32[40,4,2,8,128]{4,3,2,1,0:T(8,128)S(1)}, f32[40,4,2,8,128]{4,3,2,1,0:T(8,128)}, u32[]{:S(2)}, u32[]{:S(2)}) collective-permute-start(f32[40,4,2,8,128]{4,3,2,1,0:T(8,128)S(1)} %pad_maximum_fusion), channel_id=1, source_target_pairs={{0,8},{8,0},{16,24},{24,16},{1,9},{9,1},{17,25},{25,17},{2,10},{10... | collective-permute-start | bytes 3932168 | tf_op jit(solution)/shard_map/ppermute | solution.py:509
  110.8 24.6 %collective-permute-start.2 = (f32[38,4,2,8,128]{4,3,2,1,0:T(8,128)}, f32[38,4,2,8,128]{4,3,2,1,0:T(8,128)S(1)}, u32[]{:S(2)}, u32[]{:S(2)}) collective-permute-start(f32[38,4,2,8,128]{4,3,2,1,0:T(8,128)} %get-tuple-element.30.refs_4_), channel_id=1, source_target_pairs={{0,16},{8,24},{16,0},{24,8},{1,17},{9,25},{17,1},{25,9},{2,18},{10... | collective-permute-start | bytes 3735560 | tf_op jit(solution)/shard_map/ppermute | solution.py:552
  112.3 23.1 %collective-permute-start.1 = (f32[38,4,2,8,128]{4,3,2,1,0:T(8,128)}, f32[38,4,2,8,128]{4,3,2,1,0:T(8,128)S(1)}, u32[]{:S(2)}, u32[]{:S(2)}) collective-permute-start(f32[38,4,2,8,128]{4,3,2,1,0:T(8,128)} %get-tuple-element.30.refs_4_), channel_id=1, source_target_pairs={{0,8},{8,0},{16,24},{24,16},{1,9},{9,1},{17,25},{25,17},{2,10},{10... | collective-permute-start | bytes 3735560 | tf_op jit(solution)/shard_map/ppermute | solution.py:553
  135.4 2.9 %copy-start.1 = (f32[38,4,2,8,128]{4,3,2,1,0:T(8,128)}, f32[38,4,2,8,128]{4,3,2,1,0:T(8,128)S(1)}, u32[]{:S(2)}) copy-start(f32[38,4,2,8,128]{4,3,2,1,0:T(8,128)S(1)} %collective-permute-done.2.refs_6_) | copy-start | bytes 3735556
  135.4 2.9 %collective-permute-start.3 = (f32[38,4,2,8,128]{4,3,2,1,0:T(8,128)S(1)}, f32[38,4,2,8,128]{4,3,2,1,0:T(8,128)S(1)}, u32[]{:S(2)}, u32[]{:S(2)}) collective-permute-start(f32[38,4,2,8,128]{4,3,2,1,0:T(8,128)S(1)} %collective-permute-done.2.refs_6_), channel_id=1, source_target_pairs={{0,8},{8,0},{16,24},{24,16},{1,9},{9,1},{17,25},{25,17},{2,10},{10... | collective-permute-start | bytes 3735560 | tf_op jit(solution)/shard_map/ppermute | solution.py:553
  135.4 2.9 %copy-start.2 = (f32[38,4,2,8,128]{4,3,2,1,0:T(8,128)}, f32[38,4,2,8,128]{4,3,2,1,0:T(8,128)S(1)}, u32[]{:S(2)}) copy-start(f32[38,4,2,8,128]{4,3,2,1,0:T(8,128)S(1)} %collective-permute-done.1.refs_5_) | copy-start | bytes 3735556
  138.3 1.0 copy-start.3
